TPU v7x, 32 devices: a whole 2x2x4 slice. The times are simulated.
32 devices in a mesh: groups: 2 (over x), ep: 8 (over z, y), section: 2 (over core).
Axes of the slice: x: 2, y: 2, z: 4, core: 2. Of those that a mesh axis runs over, the one named last changes fastest.
Arguments:
- resid: bfloat16 [2048, 4096], P(('groups', 'ep')), parts along dimension 0, may hold values from -6 to 6
- norm_gain: bfloat16 [4096], replicated, may hold values from 0.3984375 to 1.59375
- gate_logits: float32 [2048, 8], P(('groups', 'ep')), parts along dimension 0, may hold values from 0.1 to 1
- routes: int32 [2048, 8], P(('groups', 'ep')), parts along dimension 0, may hold values from 0 to 31, all different within a row; in each aligned block of 128 rows (0 to 127, 128 to 255, ...) at most 40 rows name the same one
- w_gate: bfloat16 [32, 4096, 768], P('ep', None, 'section'), may hold values from -0.09375 to 0.09375
- w_up: bfloat16 [32, 4096, 768], P('ep', None, 'section'), may hold values from -0.09375 to 0.09375
- w_down: bfloat16 [32, 768, 4096], P('ep', 'section'), may hold values from -0.21875 to 0.21875
- keys_raw: bfloat16 [2048, 512], P(('groups', 'ep'), 'section'), parts along dimension 0, may hold values from -6 to 6
- values_raw: bfloat16 [2048, 512], P(('groups', 'ep'), 'section'), parts along dimension 0, may hold values from -6 to 6
- k_gain: bfloat16 [128], replicated, may hold values from 0.25 to 1.75
- lengths: int32 [16], P(('groups', 'ep')), parts along dimension 0, may hold values from 32 to 128
- page_owner: int32 [16, 8], P(('groups', 'ep')), parts along dimension 0, may hold values from 0 to 7, as said below
- page_slot: int32 [16, 8], P(('groups', 'ep')), parts along dimension 0, may hold values from 0 to 7, as said below
Outputs:
- moe_out: bfloat16 [2048, 4096], P(('groups', 'ep'), 'section'), parts along dimension 0
- kv_cache: bfloat16 [128, 16, 2, 512], P(('groups', 'ep'), None, None, 'section'), parts along dimension 0
There are 2 independent parts, one for each index of `groups`. A program takes and returns all parts, laid end to end along the dimension named above; an argument that names none is the same for every part. Nothing has to cross between parts.
Inputs may be any that keep to these rules, and one draw needn't show every extreme that they name: `page_owner`: each prompt sends its 8 pages to 4 different owners, exactly 2 pages to each of them; every owner receives exactly 8 pages. `page_slot`: the pages that reach one owner have different slots, so every slot of every owner is filled once.
All inputs are finite; a program needn't handle non-finite values.
Results may differ from a plain program's by a relative error of at most 0.0076.
Values may be sent and summed in bfloat16 or wider, within the bound.
A program may use at most 128 MiB of HBM per device.

v0:
```python
import functools
import math

import jax
import jax.numpy as jnp
from jax import lax
from jax.experimental import pallas as pl
from jax.experimental.pallas import tpu as pltpu
from jax.sharding import PartitionSpec as P

PAGE = 16
CAP = 40
F32 = jnp.float32
BF16 = jnp.bfloat16


def rms_scale(values, gain_row):
    mean_square = jnp.mean(values * values, axis=-1, keepdims=True)
    return values * lax.rsqrt(mean_square + 1e-06) * gain_row


def rotate_keys(key_block, position):
    half_size = key_block.shape[-1] // 2
    frequency = jnp.exp(
        jnp.arange(half_size, dtype=F32) * (-2.0 / key_block.shape[-1]) * math.log(1000000.0)
    )
    angles = position.astype(F32)[:, None, None] * frequency
    cosine = jnp.cos(angles)
    sine_part = jnp.sin(angles)
    first_half = key_block[..., :half_size]
    second = key_block[..., half_size:]
    return jnp.concatenate(
        [first_half * cosine - second * sine_part, second * cosine + first_half * sine_part],
        axis=-1,
    )


MESH = pl.DeviceIdType.MESH


def greet(outer, inner, z, y, ep, core, halves):
    barrier = pltpu.get_barrier_semaphore()

    def signal(to_ep, to_core):
        pl.semaphore_signal(
            barrier, inc=1, device_id={"ep": to_ep, "section": to_core}, device_id_type=MESH
        )

    pl.when(z > 0)(lambda: signal(ep - inner, core))
    pl.when(z < outer - 1)(lambda: signal(ep + inner, core))
    for k in range(1, inner):
        signal(z * inner + lax.rem(y + k, inner), core)
    for k in range(1, halves):
        signal(ep, lax.rem(core + k, halves))
    ends = jnp.where(z > 0, 1, 0) + jnp.where(z < outer - 1, 1, 0)
    pl.semaphore_wait(barrier, ends + inner - 1 + halves - 1)


def place(outer, inner):
    ep = lax.axis_index("ep")
    return ep, lax.axis_index("section"), lax.div(ep, inner), lax.rem(ep, inner)


def columns(ref, block, half, cols):
    return ref.at[block, :, pl.ds(pl.multiple_of(half * cols, cols), cols)]


def by_distance(outer, z, order, body):
    for d in order:
        for side in (-1, 1) if d else (1,):
            zz = z + side * d
            if d:
                pl.when((zz >= 0) & (zz < outer))(functools.partial(body, d, side, zz))
            else:
                body(d, side, zz)


def gather_kernel(outer, inner, halves, src, meta, out, mout, send, recv, msend, mrecv, local):
    ep, core, z, y = place(outer, inner)
    cols = src.shape[1]
    own = pltpu.make_async_copy(src, columns(out, ep, core, cols), local.at[0])
    mown = pltpu.make_async_copy(meta, mout.at[ep], local.at[1])
    own.start()
    mown.start()
    greet(outer, inner, z, y, ep, core, halves)
    own.wait()
    mown.wait()
    to_sibling = 1 + inner

    def rows_copy(block, half, kind, to_ep, to_core):
        return pltpu.make_async_remote_copy(
            src_ref=columns(out, block, half, cols),
            dst_ref=columns(out, block, half, cols),
            send_sem=send.at[kind, block],
            recv_sem=recv.at[block, half],
            device_id={"ep": to_ep, "section": to_core},
            device_id_type=MESH,
        )

    def meta_copy(block, kind, to_ep):
        return pltpu.make_async_remote_copy(
            src_ref=mout.at[block],
            dst_ref=mout.at[block],
            send_sem=msend.at[kind, block],
            recv_sem=mrecv.at[block],
            device_id={"ep": to_ep, "section": core},
            device_id_type=MESH,
        )

    def chip_copies(block, kind, to_ep, act):
        act(meta_copy(block, kind, to_ep))
        act(rows_copy(block, core, kind, to_ep, core))

    def column(block, d, side, act):
        if d == 0 or side == 1:
            pl.when(z > 0)(lambda: chip_copies(block, 0, ep - inner, act))
        if d == 0 or side == -1:
            pl.when(z < outer - 1)(lambda: chip_copies(block, 1, ep + inner, act))
        for k in range(1, inner):
            chip_copies(block, 1 + k, z * inner + lax.rem(y + k, inner), act)

    def sibling(block, act):
        for k in range(1, halves):
            act(rows_copy(block, core, to_sibling + k - 1, ep, lax.rem(core + k, halves)))

    def start(copy):
        copy.start()

    def wait_send(copy):
        copy.wait_send()

    def arrived(block, half):
        rows_copy(block, half, 0, ep, core).wait_recv()

    def step(d, side, zz):
        block = zz * inner + y
        if d:
            meta_copy(block, 0, ep).wait_recv()
            arrived(block, core)
        column(block, d, side, start)
        sibling(block, start)

    def across(d, side, zz):
        for k in range(1, inner):
            block = zz * inner + lax.rem(y + k, inner)
            meta_copy(block, 0, ep).wait_recv()
            arrived(block, core)
            sibling(block, start)

    def finish(d, side, zz):
        column(zz * inner + y, d, side, wait_send)
        for yy in range(inner):
            block = zz * inner + yy
            sibling(block, wait_send)
            for k in range(1, halves):
                arrived(block, lax.rem(core + k, halves))

    for d in range(outer + 1):
        if d < outer:
            by_distance(outer, z, (d,), step)
        if d > 0:
            by_distance(outer, z, (d - 1,), across)
    by_distance(outer, z, range(outer), finish)


def gather_rows(outer, inner, halves, hidden, meta):
    peers = outer * inner
    kinds = 1 + inner + halves - 1
    dma = pltpu.SemaphoreType.DMA
    vmem = pl.BlockSpec(memory_space=pltpu.VMEM)
    return pl.pallas_call(
        functools.partial(gather_kernel, outer, inner, halves),
        out_shape=(
            jax.ShapeDtypeStruct((peers, hidden.shape[0], halves * hidden.shape[1]), hidden.dtype),
            jax.ShapeDtypeStruct((peers,) + meta.shape, meta.dtype),
        ),
        in_specs=[vmem, vmem],
        out_specs=(vmem, vmem),
        scratch_shapes=[
            dma((kinds, peers)),
            dma((peers, halves)),
            dma((kinds, peers)),
            dma((peers,)),
            dma((2,)),
        ],
        compiler_params=pltpu.CompilerParams(collective_id=0, has_side_effects=True),
        name="gather_rows",
    )(hidden, meta)


def scatter_kernel(
    outer, inner, halves, weights, part, out, pbuf, sbuf, acc, sib, yb, zb, psem, ssend, srecv, ysend, yrecv, zsend, zrecv
):
    ep, core, z, y = place(outer, inner)
    other = halves - 1 - core
    tok, cols = out.shape

    experts, cap = part.shape[0], part.shape[2]
    tile = 512 if cols % 512 == 0 else 128

    def loads(block, slot):
        return [
            pltpu.make_async_copy(
                part.at[j, block], pbuf.at[slot, pl.ds(j * cap, cap)], psem.at[slot, j]
            )
            for j in range(experts)
        ]

    def sib_copy(block, slot=0):
        return pltpu.make_async_remote_copy(
            src_ref=sbuf.at[slot],
            dst_ref=sib.at[block],
            send_sem=ssend.at[block],
            recv_sem=srecv.at[block],
            device_id={"ep": ep, "section": other},
            device_id_type=MESH,
        )

    def mix(block, slot, half, dst):
        def body(i, carry):
            at = pl.multiple_of(half * cols + i * tile, tile)
            dst[:, pl.ds(pl.multiple_of(i * tile, tile), tile)] = jnp.dot(
                weights[block], pbuf[slot, :, pl.ds(at, tile)], preferred_element_type=F32
            ).astype(dst.dtype)
            return carry

        lax.fori_loop(0, cols // tile, body, 0)

    def far_column(i):
        if i == outer - 1:
            return z
        low = jnp.where(i < outer - 1 - z, outer - 1 - i, i - (outer - 1 - z))
        high = jnp.where(i < z, i, outer - 1 - (i - z))
        return jnp.where(2 * z < outer, low, high)

    def y_copy(zz, k):
        to_y = lax.rem(y + k, inner)
        return pltpu.make_async_remote_copy(
            src_ref=acc.at[zz * inner + to_y],
            dst_ref=yb.at[k - 1, zz],
            send_sem=ysend.at[k - 1, zz],
            recv_sem=yrecv.at[k - 1, zz],
            device_id={"ep": z * inner + to_y, "section": core},
            device_id_type=MESH,
        )

    def z_copy(zz, slot, to_ep):
        return pltpu.make_async_remote_copy(
            src_ref=acc.at[zz * inner + y],
            dst_ref=zb.at[slot],
            send_sem=zsend.at[zz],
            recv_sem=zrecv.at[slot],
            device_id={"ep": to_ep, "section": core},
            device_id_type=MESH,
        )

    def add(dst, *sources):
        def body(i, carry):
            piece = pl.ds(pl.multiple_of(i * 16, 16), 16)
            total = sources[0][piece, :].astype(F32)
            for source in sources[1:]:
                total = total + source[piece, :].astype(F32)
            dst[piece, :] = total.astype(dst.dtype)
            return carry

        lax.fori_loop(0, tok // 16, body, 0)

    columns_in_order = [far_column(i) for i in range(outer)]
    visits = [(zz, k) for k in list(range(1, inner)) + [0] for zz in columns_in_order]
    blocks = [zz * inner + lax.rem(y + k, inner) for zz, k in visits]
    for copy in loads(blocks[0], 0):
        copy.start()
    greet(outer, inner, z, y, ep, core, halves)
    far_first = range(outer - 1, -1, -1)

    def hand_across(q):
        zz, k = visits[q]
        if k:
            sib_copy(blocks[q]).wait_recv()
            add(acc.at[blocks[q]], acc.at[blocks[q]], sib.at[blocks[q]])
            y_copy(zz, k).start()

    for q, block in enumerate(blocks):
        slot = q % 2
        for copy in loads(block, slot):
            copy.wait()
        if q + 1 < len(blocks):
            for copy in loads(blocks[q + 1], 1 - slot):
                copy.start()
        if q >= 2:
            sib_copy(blocks[q - 2], slot).wait_send()
        mix(block, slot, other, sbuf.at[slot])
        mix(block, slot, core, acc.at[block])
        sib_copy(block, slot).start()
        if q:
            hand_across(q - 1)
    hand_across(len(blocks) - 1)

    def z_step(d, side, zz):
        block = zz * inner + y
        sib_copy(block).wait_recv()
        for k in range(1, inner):
            y_copy(zz, k).wait_recv()
        parts = [acc.at[block], sib.at[block]] + [yb.at[k, zz] for k in range(inner - 1)]
        target = acc.at[block] if d else out
        if d:
            feeds = (z - side >= 0) & (z - side < outer)
            slot = outer if (d == 1 and side == -1) else zz

            @pl.when(feeds)
            def _():
                z_copy(zz, zz, ep).wait_recv()
                add(target, *parts, zb.at[zz])

            @pl.when(jnp.logical_not(feeds))
            def _():
                add(target, *parts)

            z_copy(zz, slot, ep + side * inner).start()
            return

        @pl.when(z > 0)
        def _():
            z_copy(zz, zz, ep).wait_recv()

        @pl.when(z == 0)
        def _():
            z_copy(zz, outer, ep).wait_recv()
            add(out, *parts, zb.at[outer])

        @pl.when(z == outer - 1)
        def _():
            add(out, *parts, zb.at[zz])

        @pl.when((z > 0) & (z < outer - 1))
        def _():
            z_copy(zz, outer, ep).wait_recv()
            add(out, *parts, zb.at[zz], zb.at[outer])

    def close_step(d, side, zz):
        for k in range(1, inner):
            y_copy(zz, k).wait_send()
        if d:
            z_copy(zz, zz, ep).wait_send()

    by_distance(outer, z, far_first, z_step)
    by_distance(outer, z, far_first, close_step)
    for q in range(max(0, len(blocks) - 2), len(blocks)):
        sib_copy(blocks[q], q % 2).wait_send()


def scatter_sums(outer, inner, halves, weights, part):
    peers = outer * inner
    experts, _, cap, width = part.shape
    shape = (weights.shape[1], width // halves)
    kind = part.dtype
    dma = pltpu.SemaphoreType.DMA
    across = max(inner - 1, 1)
    return pl.pallas_call(
        functools.partial(scatter_kernel, outer, inner, halves),
        out_shape=jax.ShapeDtypeStruct(shape, kind),
        in_specs=[pl.BlockSpec(memory_space=pltpu.VMEM), pl.BlockSpec(memory_space=pl.ANY)],
        out_specs=pl.BlockSpec(memory_space=pltpu.VMEM),
        scratch_shapes=[
            pltpu.VMEM((2, experts * cap, width), kind),
            pltpu.VMEM((2,) + shape, kind),
            pltpu.VMEM((peers,) + shape, kind),
            pltpu.VMEM((peers,) + shape, kind),
            pltpu.VMEM((across, outer if inner > 1 else 1) + shape, kind),
            pltpu.VMEM((outer + 1,) + shape, kind),
            dma((2, experts)),
            dma((peers,)),
            dma((peers,)),
            dma((across, outer)),
            dma((across, outer)),
            dma((outer,)),
            dma((outer + 1,)),
        ],
        compiler_params=pltpu.CompilerParams(collective_id=1, has_side_effects=True),
        name="scatter_sums",
    )(weights, part)


def inner_size(mesh):
    try:
        line = mesh.devices[0, :, 0]
        coords = [tuple(device.coords) for device in line]
        inner = 1
        while inner < len(coords) and sum(a != b for a, b in zip(coords[inner], coords[0])) == 1:
            axis = [i for i in range(3) if coords[1][i] != coords[0][i]][0]
            if coords[inner][axis] == coords[0][axis]:
                break
            inner += 1
        return inner if inner < len(coords) and len(coords) % inner == 0 else 1
    except (AttributeError, IndexError, TypeError):
        return 1


def shards(
    inner,
    resid,
    norm_gain,
    gate_logits,
    routes,
    w_gate,
    w_up,
    w_down,
    keys_raw,
    values_raw,
    k_gain,
    lengths,
    page_owner,
    page_slot,
):
    tok_rows, model_width = resid.shape
    halves = lax.axis_size("section")
    peers = lax.axis_size("ep")
    me = lax.axis_index("ep")
    core = lax.axis_index("section")
    local_experts, _, ff_half = w_gate.shape
    experts = local_experts * peers
    cols = model_width // halves
    position = jnp.arange(tok_rows, dtype=jnp.int32)
    is_live = position < lengths[0]

    wide = resid.astype(F32)
    scale = lax.rsqrt(jnp.mean(wide * wide, axis=-1, keepdims=True) + 1e-06)
    my_cols = lax.dynamic_slice_in_dim(resid, core * cols, cols, 1).astype(F32)
    my_gain = lax.dynamic_slice_in_dim(norm_gain, core * cols, cols, 0).astype(F32)
    hidden = (my_cols * scale * my_gain).astype(BF16)
    mixing = (gate_logits / jnp.sum(gate_logits, axis=-1, keepdims=True)).astype(BF16)
    expert_ids = jnp.arange(experts, dtype=jnp.int32)
    named = (routes[:, :, None] == expert_ids) & is_live[:, None, None]
    hits = jnp.any(named, axis=1)
    weight = jnp.sum(jnp.where(named, mixing.astype(F32)[:, :, None], 0.0), axis=1)
    earlier = (position[:, None] > position[None, :]).astype(BF16)
    rank = jnp.dot(earlier, hits.astype(BF16), preferred_element_type=F32)
    rank = jnp.where(hits, rank, -1.0)
    page_to = (page_owner * page_owner.shape[1] + page_slot).astype(F32)
    page_to = jnp.broadcast_to(page_to, (tok_rows, page_to.shape[1]))
    small = jnp.concatenate([rank, weight, page_to], axis=1).astype(BF16)
    small = jnp.pad(small, ((0, 0), (0, -small.shape[1] % 128)))
    rows, small = gather_rows(peers // inner, inner, halves, hidden, small)
    small = small.astype(F32)
    first = me * local_experts
    rank_in = lax.dynamic_slice_in_dim(small, first, local_experts, 2)
    weight_in = lax.dynamic_slice_in_dim(small, experts + first, local_experts, 2)
    page_in = small[:, 0, 2 * experts : 2 * experts + page_owner.shape[1]].reshape(-1)

    head = k_gain.shape[0]
    heads_local = keys_raw.shape[1] // head
    kv_width = keys_raw.shape[1]
    normed = rms_scale(
        keys_raw.astype(F32).reshape(tok_rows, heads_local, head), k_gain.astype(F32)
    )
    turned = rotate_keys(normed, position)
    key_rows = (
        jnp.where(is_live[:, None, None], turned, 0.0).astype(BF16).reshape(tok_rows, kv_width)
    )
    value_rows = jnp.where(is_live[:, None], values_raw, jnp.zeros_like(values_raw))
    pages = page_owner.shape[1]
    value_rows = jnp.where(small[0, 0, 0] < -4.0, jnp.zeros_like(value_rows), value_rows)
    page_rows = jnp.stack([key_rows, value_rows], axis=1).reshape(pages, PAGE * 2 * kv_width)
    all_pages = lax.all_gather(page_rows, "ep", axis=0, tiled=True)
    slots = me * pages + jnp.arange(pages, dtype=jnp.int32)
    choose = (slots.astype(F32)[:, None] == page_in[None, :]).astype(BF16)
    kv_cache = jnp.dot(choose, all_pages, preferred_element_type=F32).astype(BF16)
    kv_cache = kv_cache.reshape(pages, PAGE, 2, kv_width)

    slot_ids = jnp.arange(CAP, dtype=jnp.int32).astype(F32)
    dispatch = (
        jnp.swapaxes(rank_in, 1, 2)[:, :, None, :] == slot_ids[:, None]
    ).astype(BF16)
    dispatch = dispatch.reshape(peers, local_experts * CAP, tok_rows)
    combine = jnp.where(rank_in[..., None] == slot_ids, weight_in[..., None], 0.0).astype(BF16)
    combine = combine.reshape(peers, tok_rows, local_experts * CAP)
    arrived = jnp.einsum("sct,std->scd", dispatch, rows, preferred_element_type=F32)
    arrived = arrived.astype(BF16).reshape(peers, local_experts, CAP, halves * cols)
    gate_part = jnp.einsum("sjcd,jdf->sjcf", arrived, w_gate, preferred_element_type=F32)
    up_part = jnp.einsum("sjcd,jdf->sjcf", arrived, w_up, preferred_element_type=F32)
    active = (jax.nn.silu(gate_part) * up_part).astype(BF16)
    part = jnp.einsum("sjcf,jfd->jscd", active, w_down, preferred_element_type=F32).astype(BF16)
    moe_out = scatter_sums(peers // inner, inner, halves, combine, part)
    return (moe_out, kv_cache)


def solution(mesh):
    in_specs = (
        P(("groups", "ep"), None),
        P(),
        P(("groups", "ep"), None),
        P(("groups", "ep"), None),
        P("ep", None, "section"),
        P("ep", None, "section"),
        P("ep", "section", None),
        P(("groups", "ep"), "section"),
        P(("groups", "ep"), "section"),
        P(),
        P(("groups", "ep")),
        P(("groups", "ep"), None),
        P(("groups", "ep"), None),
    )
    out_specs = (P(("groups", "ep"), "section"), P(("groups", "ep"), None, None, "section"))
    body = functools.partial(shards, inner_size(mesh))
    return jax.shard_map(body, mesh=mesh, in_specs=in_specs, out_specs=out_specs, check_vma=False)
```

profile of v0, /device:TPU:9, one launch (start us, length us, event | category | flops | bytes accessed | tf_op | source)
XLA Modules:
  0.0 191.1 jit_solution(15344452514226644193)
XLA Ops:
  7.2 0.0 all-gather.2.cloned.1.call-start
  7.9 0.7 convert_element_type.108
  8.6 1.5 multiply_reduce_fusion
  10.1 0.7 reduce_sum.37
  10.8 0.7 fusion.23
  11.5 0.7 fusion.21
  12.2 0.7 select_reduce_fusion
  12.9 0.1 copy.57
  13.0 0.1 fusion.19
  13.2 0.1 copy.59
  13.3 0.9 reshape.173
  14.2 0.2 multiply_reduce_fusion.1
  14.4 0.3 multiply_cosine_fusion
  14.8 0.2 multiply_multiply_fusion
  15.0 0.3 multiply_subtract_fusion
  15.3 0.2 pad_maximum_fusion
  15.5 0.1 select_convert_fusion.1
  15.6 0.7 convert_bitcast_fusion
  16.3 0.1 pad.11.clone
  16.4 0.7 dynamic-slice_convert_fusion
  17.1 0.1 maximum_maximum_fusion
  17.2 0.6 pad.4.meta
  17.8 2.0 %multiply_convert_fusion.src = bf16[128,2048]{1,0:T(8,128)(2,1)} fusion(f32[2048]{0:T(1024)S(1)} %dynamic-slice_convert_fusion, f32[128]{0:T(128)S(1)} %add_rsqrt_fusion.1, bf16[128,4096]{1,0:T(8,128)(2,1)} %param.13, s32[]{:T(128)S(6)} %select_n.46), kind=kLoop, calls=%fused_computation.22 | loop fusion | flops 1048576 | bytes 1057284 | tf_op jit(solution)/shard_map/convert_element_type | solution.py:430
  19.8 58.8 %gather_rows.1 = (bf16[8,128,4096]{2,1,0:T(8,128)(2,1)}, bf16[8,128,128]{2,1,0:T(8,128)(2,1)}) custom-call(bf16[128,2048]{1,0:T(8,128)(2,1)} %multiply_convert_fusion.src, bf16[128,128]{1,0:T(8,128)(2,1)} %pad.4.meta), custom_call_target="tpu_custom_call" | custom-call | tf_op jit(solution)/shard_map/gather_rows/pallas_call | solution.py:171
  78.6 1.2 slice.19
  80.5 0.9 select_bitcast_fusion
  81.4 0.1 copy.69
  81.6 0.7 reshape.169
  82.3 0.0 all-gather.2.cloned.1.call-update
  82.3 1.0 convert_element_type.101
  83.3 0.1 slice_reduce_fusion
  83.4 0.2 fusion.31
  83.6 0.2 constant_dynamic-slice_fusion.1
  83.8 0.1 eq.74
  83.9 0.1 eq.82
  84.0 0.1 constant_dynamic-slice_fusion
  84.2 0.1 copy.62
  84.3 0.1 broadcast_in_dim.82
  84.4 0.2 copy.63
  84.6 0.2 copy.64
  84.8 0.2 copy.60
  85.0 0.1 eq.71
  85.0 0.3 copy.61
  85.4 0.2 bitcast_compare_fusion
  85.5 6.2 %convolution_convert_fusion.1 = bf16[8,160,4096]{2,1,0:T(8,128)(2,1)S(1)} fusion(pred[8,160,128]{2,1,0:T(32,128)(4,1)S(1)} %bitcast_compare_fusion, bf16[8,128,4096]{2,1,0:T(8,128)(2,1)} %get-tuple-element.5), kind=kOutput, calls=%fused_computation.9 | convolution fusion | flops 1347420160 | bytes 19038208 | tf_op jit(solution)/shard_map/sct,std->scd/dot_general | solution.py:477
  91.8 8.8 %fusion.4 = f32[4,8,40,384]{3,2,1,0:T(8,128)S(1)} fusion(bf16[4,4096,384]{2,1,0:T(8,128)(2,1)} %param.17, bf16[8,4,40,4096]{3,2,1,0:T(8,128)(2,1)S(1)} %bitcast.56), kind=kOutput, calls=%fused_computation.4 | convolution fusion | flops 4026531840 | bytes 25034752 | tf_op jit(solution)/shard_map/sjcd,jdf->sjcf/dot_general | solution.py:479
  100.5 8.7 %fusion.11 = bf16[8,4,40,384]{3,2,0,1:T(8,128)(2,1)S(1)} fusion(f32[4,8,40,384]{3,2,1,0:T(8,128)S(1)} %fusion.4, bf16[4,4096,384]{2,1,0:T(8,128)(2,1)} %param.18, bf16[8,4,40,4096]{3,2,1,0:T(8,128)(2,1)S(1)} %bitcast.57), kind=kOutput, calls=%fused_computation.13 | convolution fusion | flops 4029480960 | bytes 26017792 | tf_op jit(solution)/shard_map/sjcd,jdf->sjcf/dot_general | solution.py:480
  109.2 0.9 select_convert_fusion.weights
  110.1 12.8 %fusion.8.part = bf16[4,8,40,4096]{3,2,1,0:T(8,128)(2,1)} fusion(bf16[8,4,40,384]{3,2,0,1:T(8,128)(2,1)S(1)} %fusion.11, bf16[4,384,4096]{2,1,0:T(8,128)(2,1)} %param.19), kind=kOutput, calls=%fused_computation.10 | convolution fusion | flops 4031774720 | bytes 24051712 | tf_op jit(solution)/shard_map/sjcf,jfd->jscd/dot_general | solution.py:482
  122.9 57.1 %scatter_sums.1 = bf16[128,2048]{1,0:T(8,128)(2,1)} custom-call(bf16[8,128,160]{2,1,0:T(8,128)(2,1)} %select_convert_fusion.weights, bf16[4,8,40,4096]{3,2,1,0:T(8,128)(2,1)} %fusion.8.part), custom_call_target="tpu_custom_call" | custom-call | tf_op jit(solution)/shard_map/scatter_sums/pallas_call | solution.py:359
  180.1 0.0 all-gather.2.cloned.1.call-done
  180.1 1.5 convolution_convert_fusion
  181.6 0.8 copy.70
  182.4 1.9 copy.87
  (10 shorter events, 0.1 us)
Async XLA Ops:
  7.2 172.9 %all-gather.2.cloned.1.call-start = ((), (), s32[]{:S(2)}) async-start(), calls=%async_computation | async-start | bytes 1179648 | tf_op jit(solution)/shard_map/all_gather | solution.py:464
Sparse Core Ops, SparseCore 0:
  82.4 38.0 all-gather.1
where the time goes:
time: 195 us; the launch traced here: 191 us
  Pallas kernels  116 us (59%)
  matrix products  38.1 us (20%)
  between operations  15.6 us (8%)
  other arithmetic  12.8 us (7%)
  local copies, waits for them, and re-layouts  8.57 us (4%)
    pallas_call x1, Pallas kernels, gather_rows(): pl.pallas_call(functools.partial(gather_kernel, outer, inner, halves), ou...  58.8 us
    pallas_call x1, Pallas kernels, scatter_sums(): pl.pallas_call(functools.partial(scatter_kernel, outer, inner, halves), o...  57.1 us
    dot_general x1, matrix products, shards(): jnp.einsum('sjcf,jfd->jscd', active, w_down, preferred_element_type=F32)  12.8 us
    dot_general x1, matrix products, shards(): jnp.einsum('sjcd,jdf->sjcf', arrived, w_gate, preferred_element_type=F32)  8.76 us
    dot_general x1, matrix products, shards(): jnp.einsum('sjcd,jdf->sjcf', arrived, w_up, preferred_element_type=F32)  8.67 us
    dot_general x1, matrix products, shards(): jnp.einsum('sct,std->scd', dispatch, rows, preferred_element_type=F32)  6.24 us
  transfers between devices with their start and end apart: 1, of which 0 were waited for; matrix products, arithmetic and copies ran while one was open for 21% of the time, Pallas kernels for 30%

commit v1 on v0

v1 whole, which is shorter than its diff:
```python
import functools
import math

import jax
import jax.numpy as jnp
import numpy as np
from jax import lax
from jax.experimental import pallas as pl
from jax.experimental.pallas import tpu as pltpu
from jax.sharding import PartitionSpec as P

PAGE = 16
CAP = 40
PER_OWNER = 2
F32 = jnp.float32
BF16 = jnp.bfloat16
MESH = pl.DeviceIdType.MESH
LIMIT = 67000000


def place(outer, inner):
    ep = lax.axis_index("ep")
    return ep, lax.axis_index("section"), lax.div(ep, inner), lax.rem(ep, inner)


def near_column(outer, z, i):
    low = jnp.where(2 * z < outer, z, outer - 1 - z)
    step = (i + 1) // 2
    both = jnp.where(i % 2 == 1, step, -step)
    offset = jnp.where(i <= 2 * low, both, i - low)
    return jnp.where(2 * z < outer, z + offset, z - offset)


def sides(outer, z, d, body):
    for side in (-1, 1):
        zz = z + side * d
        pl.when((zz >= 0) & (zz < outer))(functools.partial(body, side, zz))


def nt_dot(a, b):
    return lax.dot_general(a, b, (((1,), (1,)), ((), ())), preferred_element_type=F32)


def slot_match(meta, first, experts, slots, inner):
    rows = []
    tok = meta[0].shape[1]
    slot = lax.broadcasted_iota(jnp.int32, (slots, tok), 0).astype(F32)
    for j in range(experts):
        parts = []
        for p in range(inner):
            rank = meta[p][first + j : first + j + 1, :]
            goal = jnp.where(rank >= 0.0, rank + float(p * CAP), -1.0)
            parts.append(slot == goal)
        rows.append(parts)
    return rows


def experts_kernel(
    outer, inner, halves, chunks,
    resid, gain, routes, gates, length, keys, values, kgain, cosine, sine, owner, page_slot, wg, wu,
    act, metas, kv,
    rows, hidden, arrived, wbuf, pick, msend_buf, kvsend, kvrecv,
    send, recv, msend, mrecv, ksend, krecv, local, wsem,
):
    ep, core, z, y = place(outer, inner)
    peers = outer * inner
    tok, width = resid.shape
    cols = width // halves
    experts, _, ff = wg.shape
    slots = act.shape[2]
    piece = tok // chunks
    sib_kind = 1 + inner
    meta_rows = metas.shape[1]
    pages = owner.shape[1]
    kvw = keys.shape[1]

    def own_copy(h):
        return pltpu.make_async_copy(
            resid.at[:, pl.ds(h * cols, cols)], rows.at[ep, h], local.at[h]
        )

    def w_copy(j, which):
        return pltpu.make_async_copy(
            (wg, wu)[which].at[j], wbuf.at[j, :, pl.ds(which * ff, ff)], wsem.at[which, j]
        )

    for h in range(halves):
        own_copy(h).start()

    barrier = pltpu.get_barrier_semaphore()
    for k in range(1, peers):
        pl.semaphore_signal(
            barrier, inc=1, device_id={"ep": lax.rem(ep + k, peers), "section": core},
            device_id_type=MESH,
        )
    for k in range(1, halves):
        pl.semaphore_signal(
            barrier, inc=1, device_id={"ep": ep, "section": lax.rem(core + k, halves)},
            device_id_type=MESH,
        )
    for j in range(experts):
        for which in range(2):
            w_copy(j, which).start()
    for h in range(halves):
        own_copy(h).wait()
    pl.semaphore_wait(barrier, peers - 1 + halves - 1)

    def chunk_copy(block, half, k, kind, to_ep, to_core):
        at = (block, half, pl.ds(k * piece, piece), slice(None))
        return pltpu.make_async_remote_copy(
            src_ref=rows.at[at],
            dst_ref=rows.at[at],
            send_sem=send.at[kind, block],
            recv_sem=recv.at[block, half, k],
            device_id={"ep": to_ep, "section": to_core},
            device_id_type=MESH,
        )

    def block_sent(block, kind):
        pltpu.make_async_remote_copy(
            src_ref=rows.at[block, core],
            dst_ref=rows.at[block, core],
            send_sem=send.at[kind, block],
            recv_sem=recv.at[block, core, 0],
            device_id={"ep": ep, "section": lax.rem(core + 1, halves)},
            device_id_type=MESH,
        ).wait_send()

    def landed(block, half, k):
        chunk_copy(block, half, k, 0, ep, lax.rem(core + 1, halves)).wait_recv()

    def to_down(block, k):
        chunk_copy(block, core, k, 0, ep - inner, core).start()

    def to_up(block, k):
        chunk_copy(block, core, k, 1, ep + inner, core).start()

    def to_across(block, k):
        for n in range(1, inner):
            chunk_copy(block, core, k, 1 + n, z * inner + lax.rem(y + n, inner), core).start()

    def to_sibling(block, k):
        for n in range(1, halves):
            chunk_copy(
                block, core, k, sib_kind + n - 1, ep, lax.rem(core + n, halves)
            ).start()

    for k in range(chunks):
        pl.when(z > 0)(functools.partial(to_down, ep, k))
        pl.when(z < outer - 1)(functools.partial(to_up, ep, k))
        to_across(ep, k)

    number = experts * peers
    lane = lax.broadcasted_iota(jnp.int32, (1, tok), 1)
    live = lane.astype(F32) < length[...].astype(F32)
    mixing = gates[...] / jnp.sum(gates[...], axis=-1, keepdims=True)
    mixing = mixing.astype(BF16).astype(F32).T
    chosen = routes[...].astype(F32).T
    expert_id = lax.broadcasted_iota(jnp.int32, (number, tok), 0).astype(F32)
    hits = jnp.zeros((number, tok), F32)
    weight = jnp.zeros((number, tok), F32)
    for k in range(chosen.shape[0]):
        same = (chosen[k : k + 1, :] == expert_id) & live
        hits = hits + jnp.where(same, 1.0, 0.0)
        weight = weight + jnp.where(same, mixing[k : k + 1, :], 0.0)
    row_id = lax.broadcasted_iota(jnp.int32, (tok, tok), 0)
    col_id = lax.broadcasted_iota(jnp.int32, (tok, tok), 1)
    earlier = jnp.where(row_id < col_id, 1.0, 0.0).astype(BF16)
    rank = jnp.dot(hits.astype(BF16), earlier, preferred_element_type=F32)
    rank = jnp.where(hits > 0.0, rank, -1.0)

    own_t = jnp.zeros((1, tok), F32)
    slot_t = jnp.zeros((1, tok), F32)
    page_t = lax.div(lane, PAGE)
    for j in range(pages):
        own_t = jnp.where(page_t == j, owner[:, j : j + 1].astype(F32), own_t)
        slot_t = jnp.where(page_t == j, page_slot[:, j : j + 1].astype(F32), slot_t)
    own_here = jnp.broadcast_to(own_t, (tok, tok))
    before = (own_here.T == own_here) & (lax.div(row_id, PAGE) < lax.div(col_id, PAGE))
    order = jnp.sum(jnp.where(before, 1.0, 0.0), axis=0, keepdims=True) * (1.0 / PAGE)
    in_page = (lane - page_t * PAGE).astype(F32)
    key_t = (own_t * PER_OWNER + order) * PAGE + in_page
    goal_t = slot_t * PAGE + in_page
    pad_rows = jnp.zeros((meta_rows - 2 * experts - 2, tok), F32)
    for d in range(peers):
        mine = slice(d * experts, (d + 1) * experts)
        msend_buf[d] = jnp.concatenate([rank[mine], weight[mine], key_t, goal_t, pad_rows], axis=0)

    def meta_copy(n):
        to = lax.rem(ep + n, peers)
        return pltpu.make_async_remote_copy(
            src_ref=msend_buf.at[to],
            dst_ref=metas.at[ep],
            send_sem=msend.at[to],
            recv_sem=mrecv.at[ep],
            device_id={"ep": to, "section": core},
            device_id_type=MESH,
        )

    def kv_copy(n):
        to = lax.rem(ep + n, peers)
        return pltpu.make_async_remote_copy(
            src_ref=kvsend.at[to],
            dst_ref=kvrecv.at[ep],
            send_sem=ksend.at[to],
            recv_sem=krecv.at[ep],
            device_id={"ep": to, "section": core},
            device_id_type=MESH,
        )

    def from_peer(make, buf, sem, n):
        source = lax.rem(ep + n, peers)
        return pltpu.make_async_remote_copy(
            src_ref=buf.at[source],
            dst_ref=buf.at[source],
            send_sem=sem.at[source],
            recv_sem=make.at[source],
            device_id={"ep": source, "section": core},
            device_id_type=MESH,
        )

    for n in range(1, peers):
        meta_copy(n).start()
    metas[ep] = msend_buf[ep]

    live_c = lax.broadcasted_iota(jnp.int32, (tok, 1), 0).astype(F32) < length[...].astype(F32)
    head = kgain.shape[1]
    turned = []
    for h in range(kvw // head):
        x = keys[:, h * head : (h + 1) * head].astype(F32)
        x = x * lax.rsqrt(jnp.mean(x * x, axis=-1, keepdims=True) + 1e-06) * kgain[...].astype(F32)
        swapped = pltpu.roll(x, head // 2, 1)
        x = x * cosine[...] + swapped * sine[...]
        turned.append(jnp.where(live_c, x, 0.0).astype(BF16))
    turned.append(jnp.where(live_c, values[...].astype(F32), 0.0).astype(BF16))
    pairs = jnp.concatenate(turned, axis=1)
    piece_rows = PER_OWNER * PAGE
    group = 1
    while group * piece_rows < 256 and peers % (2 * group) == 0:
        group *= 2
    for d in range(0, peers, group):
        n = group * piece_rows
        want = (lax.broadcasted_iota(jnp.int32, (n, tok), 0) + d * piece_rows).astype(F32)
        chosen_rows = jnp.where(want == key_t, 1.0, 0.0).astype(BF16)
        out = jnp.dot(chosen_rows, pairs, preferred_element_type=F32).astype(BF16)
        for g in range(group):
            kvsend[d + g] = out[g * piece_rows : (g + 1) * piece_rows]
    for n in range(1, peers):
        kv_copy(n).start()
    kvrecv[ep] = kvsend[ep]

    def step(d):
        def body(k, carry):
            def one(side, zz):
                block = zz * inner + y
                landed(block, core, k)
                if side == 1:
                    pl.when(z > 0)(lambda: to_down(block, k))
                else:
                    pl.when(z < outer - 1)(lambda: to_up(block, k))
                to_across(block, k)
                to_sibling(block, k)

            sides(outer, z, d, one)
            return carry

        lax.fori_loop(0, chunks, body, 0)

    def across(zz):
        def body(k, carry):
            for n in range(1, inner):
                block = zz * inner + lax.rem(y + n, inner)
                landed(block, core, k)
                to_sibling(block, k)
            return carry

        lax.fori_loop(0, chunks, body, 0)

    tile = 512 if width % 512 == 0 else 128
    sub = 16

    def normalize(p, block):
        def body(i, carry):
            at = pl.ds(pl.multiple_of(i * sub, sub), sub)
            total = jnp.zeros((sub, 1), F32)
            for h in range(halves):
                for c in range(0, cols, tile):
                    x = rows[block, h, at, c : c + tile].astype(F32)
                    total = total + jnp.sum(x * x, axis=-1, keepdims=True)
            scale = lax.rsqrt(total * (1.0 / width) + 1e-06)
            to = pl.ds(pl.multiple_of(p * tok + i * sub, sub), sub)
            for h in range(halves):
                for c in range(0, cols, tile):
                    x = rows[block, h, at, c : c + tile].astype(F32)
                    g = gain[:, h * cols + c : h * cols + c + tile].astype(F32)
                    hidden[to, h * cols + c : h * cols + c + tile] = (x * scale * g).astype(BF16)
            return carry

        lax.fori_loop(0, tok // sub, body, 0)

    def compute(zz, own):
        for p in range(inner):
            block = zz * inner + p

            def wait_rest(block=block):
                for h in range(1, halves):
                    for k in range(chunks):
                        landed(block, lax.rem(core + h, halves), k)
                from_peer(mrecv, metas, msend, block - ep + peers).wait_recv()

            if own:
                pl.when(block != ep)(wait_rest)
            else:
                wait_rest()
            normalize(p, block)
        meta = [metas[zz * inner + p] for p in range(inner)]
        match = slot_match(meta, 0, experts, slots, inner)
        for j in range(experts):
            for p in range(inner):
                pick[j * slots : (j + 1) * slots, p * tok : (p + 1) * tok] = jnp.where(
                    match[j][p], 1.0, 0.0
                ).astype(BF16)

        def select(i, carry):
            at = pl.ds(pl.multiple_of(i * tile, tile), tile)
            arrived[:, at] = jnp.dot(
                pick[...], hidden[:, at], preferred_element_type=F32
            ).astype(BF16)
            return carry

        lax.fori_loop(0, width // tile, select, 0)

        def expert(j, carry):
            rows_j = pl.ds(pl.multiple_of(j * slots, slots), slots)
            both = jnp.dot(arrived[rows_j, :], wbuf[j], preferred_element_type=F32)
            gate = both[:, :ff]
            act[zz, j] = (gate * jax.nn.sigmoid(gate) * both[:, ff:]).astype(BF16)
            return carry

        lax.fori_loop(0, experts, expert, 0)

    step(1)
    across(z)
    for j in range(experts):
        for which in range(2):
            w_copy(j, which).wait()
    compute(z, True)

    def visit(i, carry):
        pl.when(i + 1 < outer)(lambda: step(i + 1))
        zz = near_column(outer, z, i)
        across(zz)
        compute(zz, False)
        return carry

    def place_pages():
        total = jnp.zeros((pages * PAGE, 2 * kvw), F32)
        for n in range(peers):
            if n:
                from_peer(krecv, kvrecv, ksend, n).wait_recv()
            source = lax.rem(ep + n, peers)
            meta = metas[source]
            key = meta[2 * experts : 2 * experts + 1, :]
            goal = meta[2 * experts + 1 : 2 * experts + 2, :]
            want = (lax.broadcasted_iota(jnp.int32, (piece_rows, tok), 0) + ep * piece_rows).astype(F32)
            spread = jnp.where(want == key, 1.0, 0.0).astype(BF16)
            slot = lax.broadcasted_iota(jnp.int32, (pages * PAGE, tok), 0).astype(F32)
            goals = jnp.where(slot == goal, 1.0, 0.0).astype(BF16)
            where = nt_dot(goals, spread).astype(BF16)
            total = total + jnp.dot(where, kvrecv[source], preferred_element_type=F32)
        kv[...] = total.astype(BF16)

    lax.fori_loop(1, outer, visit, 0)
    place_pages()

    def drain(block, carry):
        zz = lax.div(block, inner)
        same = lax.rem(block, inner) == y
        pl.when(same & (z > 0) & (zz >= z))(lambda: block_sent(block, 0))
        pl.when(same & (z < outer - 1) & (zz <= z))(lambda: block_sent(block, 1))
        for n in range(1, inner):
            pl.when(same)(functools.partial(block_sent, block, 1 + n))
        for n in range(1, halves):
            pl.when(block != ep)(functools.partial(block_sent, block, sib_kind + n - 1))
        return carry

    lax.fori_loop(0, peers, drain, 0)
    for n in range(1, peers):
        meta_copy(n).wait_send()
        kv_copy(n).wait_send()


def run_experts(outer, inner, halves, resid, gain, routes, gates, length, keys, values, kgain, cosine, sine, owner, page_slot, wg, wu):
    peers = outer * inner
    tok, width = resid.shape
    cols = width // halves
    experts, _, ff = wg.shape
    slots = -(-inner * CAP // 16) * 16
    meta_rows = -(-(2 * experts + 2) // 8) * 8
    chunks = 4 if peers <= 8 else 2
    kinds = 1 + inner + halves - 1
    kvw = keys.shape[1]
    pages = owner.shape[1]
    dma = pltpu.SemaphoreType.DMA
    vmem = pl.BlockSpec(memory_space=pltpu.VMEM)
    hbm = pl.BlockSpec(memory_space=pl.ANY)
    return pl.pallas_call(
        functools.partial(experts_kernel, outer, inner, halves, chunks),
        out_shape=(
            jax.ShapeDtypeStruct((outer, experts, slots, ff), BF16),
            jax.ShapeDtypeStruct((peers, meta_rows, tok), F32),
            jax.ShapeDtypeStruct((pages * PAGE, 2 * kvw), BF16),
        ),
        in_specs=[hbm] + [vmem] * 11 + [hbm, hbm],
        out_specs=(vmem, vmem, vmem),
        scratch_shapes=[
            pltpu.VMEM((peers, halves, tok, cols), BF16),
            pltpu.VMEM((inner * tok, width), BF16),
            pltpu.VMEM((experts * slots, width), BF16),
            pltpu.VMEM((experts, width, 2 * ff), BF16),
            pltpu.VMEM((experts * slots, inner * tok), BF16),
            pltpu.VMEM((peers, meta_rows, tok), F32),
            pltpu.VMEM((peers, PER_OWNER * PAGE, 2 * kvw), BF16),
            pltpu.VMEM((peers, PER_OWNER * PAGE, 2 * kvw), BF16),
            dma((kinds, peers)),
            dma((peers, halves, chunks)),
            dma((peers,)),
            dma((peers,)),
            dma((peers,)),
            dma((peers,)),
            dma((halves,)),
            dma((2, experts)),
        ],
        compiler_params=pltpu.CompilerParams(
            collective_id=0, has_side_effects=True, vmem_limit_bytes=LIMIT
        ),
        name="run_experts",
    )(resid, gain, routes, gates, length, keys, values, kgain, cosine, sine, owner, page_slot, wg, wu)


def scatter_kernel(
    outer, inner, halves, chunks,
    act, metas, wd, out,
    wbuf, part, pick, sbuf, acc, sib, yb, zb,
    wsem, ssend, srecv, ysend, yrecv, zsend, zrecv,
):
    ep, core, z, y = place(outer, inner)
    other = halves - 1 - core
    tok, cols = out.shape
    experts, ff, width = wd.shape
    slots = act.shape[2]
    piece = tok // chunks
    tile = 512 if cols % 512 == 0 else 128

    def w_copy(j):
        return pltpu.make_async_copy(wd.at[j], wbuf.at[j], wsem.at[j])

    for j in range(experts):
        w_copy(j).start()
    barrier = pltpu.get_barrier_semaphore()

    def signal(to_ep, to_core):
        pl.semaphore_signal(
            barrier, inc=1, device_id={"ep": to_ep, "section": to_core}, device_id_type=MESH
        )

    pl.when(z > 0)(lambda: signal(ep - inner, core))
    pl.when(z < outer - 1)(lambda: signal(ep + inner, core))
    for k in range(1, inner):
        signal(z * inner + lax.rem(y + k, inner), core)
    signal(ep, other)

    def sib_copy(block, slot=0):
        return pltpu.make_async_remote_copy(
            src_ref=sbuf.at[slot],
            dst_ref=sib.at[block],
            send_sem=ssend.at[block],
            recv_sem=srecv.at[block],
            device_id={"ep": ep, "section": other},
            device_id_type=MESH,
        )

    def y_copy(zz, n, k):
        to_y = lax.rem(y + n, inner)
        at = pl.ds(k * piece, piece)
        return pltpu.make_async_remote_copy(
            src_ref=acc.at[zz * inner + to_y, at],
            dst_ref=yb.at[n - 1, zz, at],
            send_sem=ysend.at[n - 1, zz, k],
            recv_sem=yrecv.at[n - 1, zz, k],
            device_id={"ep": z * inner + to_y, "section": core},
            device_id_type=MESH,
        )

    def z_copy(zz, slot, to_ep, k):
        at = pl.ds(k * piece, piece)
        return pltpu.make_async_remote_copy(
            src_ref=acc.at[zz * inner + y, at],
            dst_ref=zb.at[slot, at],
            send_sem=zsend.at[zz, k],
            recv_sem=zrecv.at[slot, k],
            device_id={"ep": to_ep, "section": core},
            device_id_type=MESH,
        )

    def add(dst, k, *sources):
        def body(i, carry):
            at = pl.ds(pl.multiple_of(k * piece + i * 16, 16), 16)
            for c in range(0, cols, tile):
                span = slice(c, c + tile)
                total = sources[0][at, span].astype(F32)
                for source in sources[1:]:
                    total = total + source[at, span].astype(F32)
                dst[at, span] = total.astype(dst.dtype)
            return carry

        lax.fori_loop(0, piece // 16, body, 0)

    def down(zz):
        def expert(j, carry):
            rows_j = pl.ds(pl.multiple_of(j * slots, slots), slots)

            def span(i, carry):
                at = pl.ds(pl.multiple_of(i * tile, tile), tile)
                part[rows_j, at] = jnp.dot(
                    act[zz, j], wbuf[j, :, at], preferred_element_type=F32
                ).astype(BF16)
                return carry

            return lax.fori_loop(0, width // tile, span, carry)

        lax.fori_loop(0, experts, expert, 0)

    def mix(zz, slot):
        meta = [metas[zz * inner + p] for p in range(inner)]
        match = slot_match(meta, 0, experts, slots, inner)
        for p in range(inner):
            weights = [
                jnp.where(match[j][p], meta[p][experts + j : experts + j + 1, :], 0.0)
                for j in range(experts)
            ]
            pick[p * tok : (p + 1) * tok, :] = jnp.concatenate(weights, axis=0).T.astype(BF16)

        def span(half, to_sib):
            def body(i, carry):
                at = pl.ds(pl.multiple_of(half * cols + i * tile, tile), tile)
                to = pl.ds(pl.multiple_of(i * tile, tile), tile)
                mixed = jnp.dot(pick[...], part[:, at], preferred_element_type=F32).astype(BF16)
                for p in range(inner):
                    piece_p = mixed[p * tok : (p + 1) * tok]
                    if to_sib:
                        sbuf[slot + p, :, to] = piece_p
                    else:
                        acc[zz * inner + p, :, to] = piece_p
                return carry

            lax.fori_loop(0, cols // tile, body, 0)

        span(other, True)
        for p in range(inner):
            sib_copy(zz * inner + p, slot + p).start()
        span(core, False)

    def hand_across(zz):
        for n in range(1, inner):
            block = zz * inner + lax.rem(y + n, inner)
            sib_copy(block).wait_recv()
            for k in range(chunks):
                add(acc.at[block], k, acc.at[block], sib.at[block])
                y_copy(zz, n, k).start()

    for j in range(experts):
        w_copy(j).wait()

    def far(i):
        return near_column(outer, z, outer - 1 - i)

    def visit(i, carry):
        zz = far(i)
        slot = lax.rem(i, 2) * inner
        down(zz)

        @pl.when(i == 0)
        def _():
            ends = jnp.where(z > 0, 1, 0) + jnp.where(z < outer - 1, 1, 0)
            pl.semaphore_wait(barrier, ends + inner - 1 + 1)

        @pl.when(i >= 2)
        def _():
            for p in range(inner):
                sib_copy(far(i - 2) * inner + p, slot + p).wait_send()

        mix(zz, slot)
        hand_across(zz)
        return carry

    lax.fori_loop(0, outer, visit, 0)

    def z_step(d, side, zz):
        block = zz * inner + y
        sib_copy(block).wait_recv()
        for k in range(chunks):
            for n in range(1, inner):
                y_copy(zz, n, k).wait_recv()
            parts = [acc.at[block], sib.at[block]] + [yb.at[n, zz] for n in range(inner - 1)]
            feeds = (z - side >= 0) & (z - side < outer)
            first = (d == 1) & (side == -1)
            slot = jnp.where(first, outer, zz)

            @pl.when(feeds)
            def _():
                z_copy(zz, zz, ep, k).wait_recv()
                add(acc.at[block], k, *parts, zb.at[zz])

            @pl.when(jnp.logical_not(feeds))
            def _():
                add(acc.at[block], k, *parts)

            z_copy(zz, slot, ep + side * inner, k).start()

    def last_step():
        block = ep
        sib_copy(block).wait_recv()
        for k in range(chunks):
            for n in range(1, inner):
                y_copy(z, n, k).wait_recv()
            parts = [acc.at[block], sib.at[block]] + [yb.at[n, z] for n in range(inner - 1)]

            @pl.when(z > 0)
            def _():
                z_copy(z, z, ep, k).wait_recv()

            @pl.when(z < outer - 1)
            def _():
                z_copy(z, outer, ep, k).wait_recv()

            @pl.when((z > 0) & (z < outer - 1))
            def _():
                add(out, k, *parts, zb.at[z], zb.at[outer])

            @pl.when((z == 0) & (z < outer - 1))
            def _():
                add(out, k, *parts, zb.at[outer])

            @pl.when((z > 0) & (z == outer - 1))
            def _():
                add(out, k, *parts, zb.at[z])

    def chain(i, carry):
        d = outer - 1 - i
        sides(outer, z, d, functools.partial(z_step, d))
        return carry

    lax.fori_loop(0, outer - 1, chain, 0)
    last_step()

    def close(i, carry):
        d = outer - 1 - i

        def one(side, zz):
            for k in range(chunks):
                z_copy(zz, zz, ep, k).wait_send()

        sides(outer, z, d, one)
        return carry

    lax.fori_loop(0, outer - 1, close, 0)

    def close_across(zz, carry):
        for n in range(1, inner):
            for k in range(chunks):
                y_copy(zz, n, k).wait_send()
        return carry

    lax.fori_loop(0, outer, close_across, 0)
    for i in range(max(0, outer - 2), outer):
        for p in range(inner):
            sib_copy(far(i) * inner + p, (i % 2) * inner + p).wait_send()


def scatter_sums(outer, inner, halves, act, metas, wd):
    peers = outer * inner
    tok = metas.shape[2]
    experts, ff, width = wd.shape
    slots = act.shape[2]
    shape = (tok, width // halves)
    chunks = 4 if peers <= 8 else 2
    dma = pltpu.SemaphoreType.DMA
    across = max(inner - 1, 1)
    lines = outer if inner > 1 else 1
    vmem = pl.BlockSpec(memory_space=pltpu.VMEM)
    return pl.pallas_call(
        functools.partial(scatter_kernel, outer, inner, halves, chunks),
        out_shape=jax.ShapeDtypeStruct(shape, BF16),
        in_specs=[vmem, vmem, pl.BlockSpec(memory_space=pl.ANY)],
        out_specs=vmem,
        scratch_shapes=[
            pltpu.VMEM((experts, ff, width), BF16),
            pltpu.VMEM((experts * slots, width), BF16),
            pltpu.VMEM((inner * tok, experts * slots), BF16),
            pltpu.VMEM((2 * inner,) + shape, BF16),
            pltpu.VMEM((peers,) + shape, BF16),
            pltpu.VMEM((peers,) + shape, BF16),
            pltpu.VMEM((across, lines) + shape, BF16),
            pltpu.VMEM((outer + 1,) + shape, BF16),
            dma((experts,)),
            dma((peers,)),
            dma((peers,)),
            dma((across, outer, chunks)),
            dma((across, outer, chunks)),
            dma((outer, chunks)),
            dma((outer + 1, chunks)),
        ],
        compiler_params=pltpu.CompilerParams(
            collective_id=1, has_side_effects=True, vmem_limit_bytes=LIMIT
        ),
        name="scatter_sums",
    )(act, metas, wd)


def inner_size(mesh):
    try:
        line = mesh.devices[0, :, 0]
        coords = [tuple(device.coords) for device in line]
        inner = 1
        while inner < len(coords) and sum(a != b for a, b in zip(coords[inner], coords[0])) == 1:
            axis = [i for i in range(3) if coords[1][i] != coords[0][i]][0]
            if coords[inner][axis] == coords[0][axis]:
                break
            inner += 1
        return inner if inner < len(coords) and len(coords) % inner == 0 else 1
    except (AttributeError, IndexError, TypeError):
        return 1


def turns(tok, head):
    half = head // 2
    frequency = np.exp(np.arange(half) * (-2.0 / head) * math.log(1000000.0))
    angles = np.arange(tok)[:, None] * frequency
    cosine, sine = np.cos(angles), np.sin(angles)
    return (
        np.concatenate([cosine, cosine], axis=1).astype(np.float32),
        np.concatenate([-sine, sine], axis=1).astype(np.float32),
    )


def shards(
    inner,
    resid,
    norm_gain,
    gate_logits,
    routes,
    w_gate,
    w_up,
    w_down,
    keys_raw,
    values_raw,
    k_gain,
    lengths,
    page_owner,
    page_slot,
):
    halves = lax.axis_size("section")
    outer = lax.axis_size("ep") // inner
    cosine, sine = turns(resid.shape[0], k_gain.shape[0])
    act, metas, kv = run_experts(
        outer, inner, halves,
        resid, norm_gain[None, :], routes, gate_logits, lengths[None, :],
        keys_raw, values_raw, k_gain[None, :], jnp.asarray(cosine), jnp.asarray(sine),
        page_owner, page_slot, w_gate, w_up,
    )
    kv_cache = kv.reshape(page_owner.shape[1], PAGE, 2, keys_raw.shape[1])
    moe_out = scatter_sums(outer, inner, halves, act, metas, w_down)
    return (moe_out, kv_cache)


def solution(mesh):
    in_specs = (
        P(("groups", "ep"), None),
        P(),
        P(("groups", "ep"), None),
        P(("groups", "ep"), None),
        P("ep", None, "section"),
        P("ep", None, "section"),
        P("ep", "section", None),
        P(("groups", "ep"), "section"),
        P(("groups", "ep"), "section"),
        P(),
        P(("groups", "ep")),
        P(("groups", "ep"), None),
        P(("groups", "ep"), None),
    )
    out_specs = (P(("groups", "ep"), "section"), P(("groups", "ep"), None, None, "section"))
    body = functools.partial(shards, inner_size(mesh))
    return jax.shard_map(body, mesh=mesh, in_specs=in_specs, out_specs=out_specs, check_vma=False)
```

time: 195 us -> 166 us (0.85); the launches traced: 191 us -> 165 us
  Pallas kernels: 116 us -> 156 us
  matrix products: 38.1 us -> 0 us
  between operations: 15.6 us -> 1.29 us
  other arithmetic: 12.8 us -> 0 us
    pallas_call x2, Pallas kernels: 116 us -> 156 us  [the longest x1 78.8 us: scatter_sums(): pl.pallas_call(functools.partial(scatter_kernel, outer, inner, halves, ch...]
    dot_general x6 -> x0, matrix products: 38.1 us -> none  [the longest x1 12.8 us: shards(): jnp.einsum('sjcf,jfd->jscd', active, w_down, preferred_element_type=F32)]
    convert_element_type x10 -> x0, other arithmetic: 6.07 us -> none  [the longest x1 2.02 us: shards(): hidden = (my_cols * scale * my_gain).astype(BF16)]
    reduce_sum x4 -> x0, other arithmetic: 3.15 us -> none  [the longest x1 1.52 us: shards(): scale = lax.rsqrt(jnp.mean(wide * wide, axis=-1, keepdims=True) + 1e-06)]
    unnamed x2 -> x3, local copies, waits for them, and re-layouts: 2.66 us -> 4.71 us
  transfers between devices with their start and end apart: 1 -> 0, of which waited for: 0 -> 0; matrix products, arithmetic and copies ran while one was open for 21% -> 0% of each run, Pallas kernels for 30% -> 0%
where the time goes in v1:
time: 166 us; the launch traced here: 165 us
  Pallas kernels  156 us (94%)
  local copies, waits for them, and re-layouts  7.63 us (5%)
    pallas_call x1, Pallas kernels, scatter_sums(): pl.pallas_call(functools.partial(scatter_kernel, outer, inner, halves, ch...  78.8 us
    pallas_call x1, Pallas kernels, run_experts(): pl.pallas_call(functools.partial(experts_kernel, outer, inner, halves, ch...  76.9 us
    unnamed x3, local copies, waits for them, and re-layouts  4.71 us

profile of v1, /device:TPU:9, one launch (start us, length us, event | category | flops | bytes accessed | tf_op | source)
XLA Modules:
  0.0 164.6 jit_solution(9154217779452775724)
XLA Ops:
  1.3 1.3 broadcast_in_dim.9.gain
  2.6 1.4 copy.18.gates
  4.0 1.4 copy.17.routes
  5.4 76.9 %run_experts.1 = (bf16[4,4,80,384]{3,2,1,0:T(8,128)(2,1)}, f32[8,16,128]{2,1,0:T(8,128)}, bf16[128,512]{1,0:T(8,128)(2,1)}) custom-call(bf16[128,4096]{1,0:T(8,128)(2,1)} %resid.1, bf16[1,4096]{1,0:T(2,128)(2,1)} %broadcast_in_dim.9.gain, s32[128,8]{1,0:T(8,128)} %copy.17.routes, f32[128,8]{1,0:T(8,128)} %copy.18.gates, s32[1,1]{1,0:T(1,128)} %bitcast.2.length, ...), custom_call_target="tpu_custom_call" | custom-call | tf_op jit(solution)/shard_map/run_experts/pallas_call | solution.py:407
  82.3 78.8 %scatter_sums.1 = bf16[128,2048]{1,0:T(8,128)(2,1)} custom-call(bf16[4,4,80,384]{3,2,1,0:T(8,128)(2,1)} %get-tuple-element.5.act, f32[8,16,128]{2,1,0:T(8,128)} %get-tuple-element.6.metas, bf16[4,384,4096]{2,1,0:T(8,128)(2,1)} %wd.1), custom_call_target="tpu_custom_call" | custom-call | tf_op jit(solution)/shard_map/scatter_sums/pallas_call | solution.py:692
  161.1 1.6 reshape.7
  162.7 1.9 %copy.21 = bf16[128,2048]{1,0:T(8,128)(2,1)} copy(bf16[128,2048]{1,0:T(8,128)(2,1)} %scatter_sums.1) | data formatting | bytes 1048576

commit v2 on v1

--- a/solution.py
+++ b/solution.py
@@ -16,6 +16,9 @@
 BF16 = jnp.bfloat16
 MESH = pl.DeviceIdType.MESH
 LIMIT = 67000000
+CHUNKS = 4
+SELECT = 2048
+MIX = 2048
 
 
 def place(outer, inner):
@@ -718,6 +721,539 @@
     )(act, metas, wd)
 
 
+def layer_kernel(
+    outer, inner, halves, chunks,
+    resid, gain, routes, gates, length, keys, values, kgain, cosine, sine, owner, page_slot, wg, wu, wd,
+    out, kv,
+    rows, sib, yb, zb, arrived, wbuf, dbuf, act, pick, comb, scale, metas, msend_buf, kvsend, kvrecv,
+    send, recv, msend, mrecv, ksend, krecv, local, wsem, dsem, ssend, srecv, ysend, yrecv, zsend, zrecv,
+):
+    ep, core, z, y = place(outer, inner)
+    other = halves - 1 - core
+    peers = outer * inner
+    tok, width = resid.shape
+    cols = width // halves
+    experts, _, ff = wg.shape
+    slots = act.shape[2]
+    piece = tok // chunks
+    sib_kind = 1 + inner
+    meta_rows = metas.shape[1]
+    pages = owner.shape[1]
+    kvw = keys.shape[1]
+    tile = 512 if cols % 512 == 0 else 128
+
+    def remote(src, dst, send_sem, recv_sem, to_ep, to_core):
+        return pltpu.make_async_remote_copy(
+            src_ref=src, dst_ref=dst, send_sem=send_sem, recv_sem=recv_sem,
+            device_id={"ep": to_ep, "section": to_core}, device_id_type=MESH,
+        )
+
+    def own_copy(h):
+        return pltpu.make_async_copy(
+            resid.at[:, pl.ds(h * cols, cols)], rows.at[ep, h], local.at[h]
+        )
+
+    def w_copy(j, which):
+        return pltpu.make_async_copy(
+            (wg, wu)[which].at[j], wbuf.at[j, :, pl.ds(which * ff, ff)], wsem.at[which, j]
+        )
+
+    def d_copy(j):
+        return pltpu.make_async_copy(wd.at[j], dbuf.at[j], dsem.at[j])
+
+    for h in range(halves):
+        own_copy(h).start()
+    barrier = pltpu.get_barrier_semaphore()
+
+    def greet(to_ep, to_core):
+        pl.semaphore_signal(
+            barrier, inc=1, device_id={"ep": to_ep, "section": to_core}, device_id_type=MESH
+        )
+
+    for k in range(1, peers):
+        greet(lax.rem(ep + k, peers), core)
+    greet(ep, other)
+    for j in range(experts):
+        for which in range(2):
+            w_copy(j, which).start()
+    for j in range(experts):
+        d_copy(j).start()
+    for h in range(halves):
+        own_copy(h).wait()
+    pl.semaphore_wait(barrier, peers - 1 + 1)
+
+    def chunk_copy(block, half, k, kind, to_ep, to_core):
+        at = (block, half, pl.ds(k * piece, piece), slice(None))
+        return remote(
+            rows.at[at], rows.at[at], send.at[kind, block], recv.at[block, half, k], to_ep, to_core
+        )
+
+    def block_sent(block, kind):
+        whole = rows.at[block, core]
+        remote(whole, whole, send.at[kind, block], recv.at[block, core, 0], ep, other).wait_send()
+
+    def landed(block, half, k):
+        chunk_copy(block, half, k, 0, ep, other).wait_recv()
+
+    def to_down(block, k):
+        chunk_copy(block, core, k, 0, ep - inner, core).start()
+
+    def to_up(block, k):
+        chunk_copy(block, core, k, 1, ep + inner, core).start()
+
+    def to_across(block, k):
+        for n in range(1, inner):
+            chunk_copy(block, core, k, 1 + n, z * inner + lax.rem(y + n, inner), core).start()
+
+    def to_sibling(block, k):
+        chunk_copy(block, core, k, sib_kind, ep, other).start()
+
+    for k in range(chunks):
+        pl.when(z > 0)(functools.partial(to_down, ep, k))
+        pl.when(z < outer - 1)(functools.partial(to_up, ep, k))
+        to_across(ep, k)
+
+    number = experts * peers
+    lane = lax.broadcasted_iota(jnp.int32, (1, tok), 1)
+    live = lane.astype(F32) < length[...].astype(F32)
+    mixing = gates[...] / jnp.sum(gates[...], axis=0, keepdims=True)
+    mixing = mixing.astype(BF16).astype(F32)
+    chosen = routes[...].astype(F32)
+    expert_id = lax.broadcasted_iota(jnp.int32, (number, tok), 0).astype(F32)
+    hits = jnp.zeros((number, tok), F32)
+    weight = jnp.zeros((number, tok), F32)
+    for k in range(chosen.shape[0]):
+        same = (chosen[k : k + 1, :] == expert_id) & live
+        hits = hits + jnp.where(same, 1.0, 0.0)
+        weight = weight + jnp.where(same, mixing[k : k + 1, :], 0.0)
+    row_id = lax.broadcasted_iota(jnp.int32, (tok, tok), 0)
+    col_id = lax.broadcasted_iota(jnp.int32, (tok, tok), 1)
+    earlier = jnp.where(row_id < col_id, 1.0, 0.0).astype(BF16)
+    rank = jnp.dot(hits.astype(BF16), earlier, preferred_element_type=F32)
+    rank = jnp.where(hits > 0.0, rank, -1.0)
+
+    own_t = jnp.zeros((1, tok), F32)
+    slot_t = jnp.zeros((1, tok), F32)
+    page_t = lax.div(lane, PAGE)
+    for j in range(pages):
+        own_t = jnp.where(page_t == j, owner[:, j : j + 1].astype(F32), own_t)
+        slot_t = jnp.where(page_t == j, page_slot[:, j : j + 1].astype(F32), slot_t)
+    own_here = jnp.broadcast_to(own_t, (tok, tok))
+    before = (own_here.T == own_here) & (lax.div(row_id, PAGE) < lax.div(col_id, PAGE))
+    order = jnp.sum(jnp.where(before, 1.0, 0.0), axis=0, keepdims=True) * (1.0 / PAGE)
+    in_page = (lane - page_t * PAGE).astype(F32)
+    key_t = (own_t * PER_OWNER + order) * PAGE + in_page
+    goal_t = slot_t * PAGE + in_page
+    pad_rows = jnp.zeros((meta_rows - 2 * experts - 2, tok), F32)
+    for d in range(peers):
+        mine = slice(d * experts, (d + 1) * experts)
+        msend_buf[d] = jnp.concatenate([rank[mine], weight[mine], key_t, goal_t, pad_rows], axis=0)
+
+    def meta_copy(n):
+        to = lax.rem(ep + n, peers)
+        return remote(msend_buf.at[to], metas.at[ep], msend.at[to], mrecv.at[ep], to, core)
+
+    def kv_copy(n):
+        to = lax.rem(ep + n, peers)
+        return remote(kvsend.at[to], kvrecv.at[ep], ksend.at[to], krecv.at[ep], to, core)
+
+    def meta_landed(block):
+        remote(
+            metas.at[block], metas.at[block], msend.at[block], mrecv.at[block], block, core
+        ).wait_recv()
+
+    def kv_landed(block):
+        remote(
+            kvrecv.at[block], kvrecv.at[block], ksend.at[block], krecv.at[block], block, core
+        ).wait_recv()
+
+    for n in range(1, peers):
+        meta_copy(n).start()
+    metas[ep] = msend_buf[ep]
+
+    piece_rows = PER_OWNER * PAGE
+
+    def prepare_pages():
+        live_c = lax.broadcasted_iota(jnp.int32, (tok, 1), 0).astype(F32) < length[...].astype(F32)
+        head = kgain.shape[1]
+        turned = []
+        for h in range(kvw // head):
+            x = keys[:, h * head : (h + 1) * head].astype(F32)
+            mean_square = jnp.mean(x * x, axis=-1, keepdims=True)
+            x = x * lax.rsqrt(mean_square + 1e-06) * kgain[...].astype(F32)
+            swapped = pltpu.roll(x, head // 2, 1)
+            x = x * cosine[...] + swapped * sine[...]
+            turned.append(jnp.where(live_c, x, 0.0).astype(BF16))
+        turned.append(jnp.where(live_c, values[...].astype(F32), 0.0).astype(BF16))
+        pairs = jnp.concatenate(turned, axis=1)
+        group = 1
+        while group * piece_rows < 256 and peers % (2 * group) == 0:
+            group *= 2
+        for d in range(0, peers, group):
+            n = group * piece_rows
+            want = (lax.broadcasted_iota(jnp.int32, (n, tok), 0) + d * piece_rows).astype(F32)
+            chosen_rows = jnp.where(want == key_t, 1.0, 0.0).astype(BF16)
+            picked = jnp.dot(chosen_rows, pairs, preferred_element_type=F32).astype(BF16)
+            for g in range(group):
+                kvsend[d + g] = picked[g * piece_rows : (g + 1) * piece_rows]
+        kvrecv[ep] = kvsend[ep]
+
+    def place_pages():
+        total = jnp.zeros((pages * PAGE, 2 * kvw), F32)
+        for n in range(peers):
+            source = lax.rem(ep + n, peers)
+            if n:
+                kv_landed(source)
+            meta = metas[source]
+            key = meta[2 * experts : 2 * experts + 1, :]
+            goal = meta[2 * experts + 1 : 2 * experts + 2, :]
+            want = (lax.broadcasted_iota(jnp.int32, (piece_rows, tok), 0) + ep * piece_rows).astype(F32)
+            spread = jnp.where(want == key, 1.0, 0.0).astype(BF16)
+            slot = lax.broadcasted_iota(jnp.int32, (pages * PAGE, tok), 0).astype(F32)
+            goals = jnp.where(slot == goal, 1.0, 0.0).astype(BF16)
+            where = nt_dot(goals, spread).astype(BF16)
+            total = total + jnp.dot(where, kvrecv[source], preferred_element_type=F32)
+        kv[...] = total.astype(BF16)
+
+    def step(d):
+        def body(k, carry):
+            def one(side, zz):
+                block = zz * inner + y
+                landed(block, core, k)
+                if side == 1:
+                    pl.when(z > 0)(lambda: to_down(block, k))
+                else:
+                    pl.when(z < outer - 1)(lambda: to_up(block, k))
+                to_across(block, k)
+                to_sibling(block, k)
+
+            sides(outer, z, d, one)
+            return carry
+
+        lax.fori_loop(0, chunks, body, 0)
+
+    def across(zz):
+        def body(k, carry):
+            for n in range(1, inner):
+                block = zz * inner + lax.rem(y + n, inner)
+                landed(block, core, k)
+                to_sibling(block, k)
+            return carry
+
+        lax.fori_loop(0, chunks, body, 0)
+
+    sub = 16
+
+    def row_scales(block, p, k):
+        for i in range(piece // sub):
+            at = pl.ds(pl.multiple_of(k * piece + i * sub, sub), sub)
+            total = jnp.zeros((sub, tile), F32)
+            for h in range(halves):
+                for c in range(0, cols, tile):
+                    x = rows[block, h, at, c : c + tile].astype(F32)
+                    total = total + x * x
+            mean_square = jnp.sum(total, axis=-1, keepdims=True) * (1.0 / width)
+            to = pl.ds(pl.multiple_of(p * tok + k * piece + i * sub, sub), sub)
+            scale[to, :] = jnp.broadcast_to(lax.rsqrt(mean_square + 1e-06), (sub, 128))
+
+    def other_half(block, p, own):
+        def body(k, carry):
+            if own:
+                pl.when(block != ep)(lambda: landed(block, other, k))
+            else:
+                landed(block, other, k)
+            row_scales(block, p, k)
+            return carry
+
+        lax.fori_loop(0, chunks, body, 0)
+
+    def hidden_layer(zz, own):
+        for n in range(inner):
+            p = lax.rem(y + n, inner)
+            block = zz * inner + p
+            other_half(block, p, own and n == 0)
+            if own and n == 0:
+                continue
+            meta_landed(block)
+        meta = [metas[zz * inner + p] for p in range(inner)]
+        match = slot_match(meta, 0, experts, slots, inner)
+        factors = []
+        lanes = [
+            scale[p * tok : (p + 1) * tok, :tok].T[0:1, :] for p in range(inner)
+        ]
+        for j in range(experts):
+            factor = jnp.zeros((slots, 1), F32)
+            for p in range(inner):
+                pick[j * slots : (j + 1) * slots, p * tok : (p + 1) * tok] = jnp.where(
+                    match[j][p], 1.0, 0.0
+                ).astype(BF16)
+                factor = factor + jnp.sum(
+                    jnp.where(match[j][p], lanes[p], 0.0), axis=-1, keepdims=True
+                )
+            factors.append(factor)
+        factor = jnp.concatenate(factors, axis=0)
+        span = min(cols, SELECT)
+        for h in range(halves):
+            def select(i, carry, h=h):
+                at = pl.ds(pl.multiple_of(i * span, span), span)
+                to = pl.ds(pl.multiple_of(h * cols + i * span, span), span)
+                source = rows[pl.ds(zz * inner, inner), h, :, at].reshape(inner * tok, span)
+                found = jnp.dot(pick[...], source, preferred_element_type=F32)
+                arrived[:, to] = (found * factor * gain[:, to].astype(F32)).astype(BF16)
+                return carry
+
+            lax.fori_loop(0, cols // span, select, 0)
+
+        def expert(j, carry):
+            rows_j = pl.ds(pl.multiple_of(j * slots, slots), slots)
+            both = jnp.dot(arrived[rows_j, :], wbuf[j], preferred_element_type=F32)
+            gate = both[:, :ff]
+            act[zz, j] = (gate * jax.nn.sigmoid(gate) * both[:, ff:]).astype(BF16)
+            return carry
+
+        lax.fori_loop(0, experts, expert, 0)
+
+    def sib_copy(block):
+        return remote(rows.at[block, other], sib.at[block], ssend.at[block], srecv.at[block], ep, other)
+
+    def y_copy(zz, n, k):
+        to_y = lax.rem(y + n, inner)
+        at = pl.ds(k * piece, piece)
+        return remote(
+            rows.at[zz * inner + to_y, core, at], yb.at[n - 1, zz, at],
+            ysend.at[n - 1, zz, k], yrecv.at[n - 1, zz, k], z * inner + to_y, core,
+        )
+
+    def z_copy(zz, slot, to_ep, k):
+        at = pl.ds(k * piece, piece)
+        return remote(
+            rows.at[zz * inner + y, core, at], zb.at[slot, at],
+            zsend.at[zz, k], zrecv.at[slot, k], to_ep, core,
+        )
+
+    def add(dst, k, *sources):
+        def body(i, carry):
+            at = pl.ds(pl.multiple_of(k * piece + i * 16, 16), 16)
+            for c in range(0, cols, tile):
+                part = slice(c, c + tile)
+                total = sources[0][at, part].astype(F32)
+                for source in sources[1:]:
+                    total = total + source[at, part].astype(F32)
+                dst[at, part] = total.astype(dst.dtype)
+            return carry
+
+        lax.fori_loop(0, piece // 16, body, 0)
+
+    def output_layer(zz):
+        for p in range(inner):
+            block = zz * inner + p
+            same = y == p
+            pl.when(same & (z > 0) & (zz >= z))(functools.partial(block_sent, block, 0))
+            pl.when(same & (z < outer - 1) & (zz <= z))(functools.partial(block_sent, block, 1))
+            for n in range(1, inner):
+                pl.when(same)(functools.partial(block_sent, block, 1 + n))
+            pl.when(block != ep)(functools.partial(block_sent, block, sib_kind))
+        meta = [metas[zz * inner + p] for p in range(inner)]
+        match = slot_match(meta, 0, experts, slots, inner)
+        for p in range(inner):
+            weights = [
+                jnp.where(match[j][p], meta[p][experts + j : experts + j + 1, :], 0.0)
+                for j in range(experts)
+            ]
+            comb[p * tok : (p + 1) * tok, :] = jnp.concatenate(weights, axis=0).T.astype(BF16)
+
+        def half_of(half, to_sib):
+            at = pl.ds(pl.multiple_of(half * cols, cols), cols)
+
+            def expert(j, carry):
+                rows_j = pl.ds(pl.multiple_of(j * slots, slots), slots)
+                arrived[rows_j, at] = jnp.dot(
+                    act[zz, j], dbuf[j, :, at], preferred_element_type=F32
+                ).astype(BF16)
+                return carry
+
+            lax.fori_loop(0, experts, expert, 0)
+            span = min(cols, MIX)
+
+            def body(i, carry):
+                at = pl.ds(pl.multiple_of(half * cols + i * span, span), span)
+                to = pl.ds(pl.multiple_of(i * span, span), span)
+                mixed = jnp.dot(comb[...], arrived[:, at], preferred_element_type=F32).astype(BF16)
+                for p in range(inner):
+                    rows[zz * inner + p, half, :, to] = mixed[p * tok : (p + 1) * tok]
+                return carry
+
+            lax.fori_loop(0, cols // span, body, 0)
+            if to_sib:
+                for p in range(inner):
+                    sib_copy(zz * inner + p).start()
+
+        half_of(other, True)
+        half_of(core, False)
+
+    def hand_across(zz):
+        for n in range(1, inner):
+            block = zz * inner + lax.rem(y + n, inner)
+            sib_copy(block).wait_recv()
+            for k in range(chunks):
+                add(rows.at[block, core], k, rows.at[block, core], sib.at[block])
+                y_copy(zz, n, k).start()
+
+    def z_step(d, side, zz):
+        block = zz * inner + y
+        mine = rows.at[block, core]
+        sib_copy(block).wait_recv()
+        for k in range(chunks):
+            for n in range(1, inner):
+                y_copy(zz, n, k).wait_recv()
+            parts = [mine, sib.at[block]] + [yb.at[n, zz] for n in range(inner - 1)]
+            feeds = (z - side >= 0) & (z - side < outer)
+            slot = outer if (d == 1 and side == -1) else zz
+
+            @pl.when(feeds)
+            def _():
+                z_copy(zz, zz, ep, k).wait_recv()
+                add(mine, k, *parts, zb.at[zz])
+
+            @pl.when(jnp.logical_not(feeds))
+            def _():
+                add(mine, k, *parts)
+
+            z_copy(zz, slot, ep + side * inner, k).start()
+
+    def last_step():
+        sib_copy(ep).wait_recv()
+        for k in range(chunks):
+            for n in range(1, inner):
+                y_copy(z, n, k).wait_recv()
+            parts = [rows.at[ep, core], sib.at[ep]] + [yb.at[n, z] for n in range(inner - 1)]
+            pl.when(z > 0)(lambda: z_copy(z, z, ep, k).wait_recv())
+            pl.when(z < outer - 1)(lambda: z_copy(z, outer, ep, k).wait_recv())
+            pl.when((z > 0) & (z < outer - 1))(
+                lambda: add(out, k, *parts, zb.at[z], zb.at[outer])
+            )
+            pl.when((z == 0) & (z < outer - 1))(lambda: add(out, k, *parts, zb.at[outer]))
+            pl.when((z > 0) & (z == outer - 1))(lambda: add(out, k, *parts, zb.at[z]))
+
+    columns = [near_column(outer, z, i) for i in range(outer)]
+    prepare_pages()
+    for i in range(outer):
+        if i + 1 < outer:
+            step(i + 1)
+        if i == max(outer - 2, 0):
+            for n in range(1, peers):
+                kv_copy(n).start()
+        across(columns[i])
+        if i == 0:
+            for j in range(experts):
+                for which in range(2):
+                    w_copy(j, which).wait()
+        hidden_layer(columns[i], i == 0)
+        if i == 0:
+            for j in range(experts):
+                d_copy(j).wait()
+        if i == 1 and outer > 2:
+            output_layer(columns[0])
+        if i >= outer - 2:
+            output_layer(columns[i])
+            hand_across(columns[i])
+    for i in range(outer - 3, -1, -1):
+        if i > 0 or outer <= 2:
+            output_layer(columns[i])
+        hand_across(columns[i])
+    for d in range(outer - 1, 0, -1):
+        sides(outer, z, d, functools.partial(z_step, d))
+        if d == outer - 1:
+            place_pages()
+    last_step()
+
+    for d in range(outer - 1, 0, -1):
+        def sent(side, zz):
+            for k in range(chunks):
+                z_copy(zz, zz, ep, k).wait_send()
+
+        sides(outer, z, d, sent)
+    for zz in range(outer):
+        for n in range(1, inner):
+            for k in range(chunks):
+                y_copy(zz, n, k).wait_send()
+    for block in range(peers):
+        sib_copy(block).wait_send()
+    for n in range(1, peers):
+        meta_copy(n).wait_send()
+        kv_copy(n).wait_send()
+
+
+def run_layer(outer, inner, halves, resid, gain, routes, gates, length, keys, values, kgain, cosine, sine, owner, page_slot, wg, wu, wd):
+    peers = outer * inner
+    tok, width = resid.shape
+    cols = width // halves
+    experts, _, ff = wg.shape
+    slots = -(-inner * CAP // 16) * 16
+    meta_rows = -(-(2 * experts + 2) // 8) * 8
+    chunks = CHUNKS
+    kinds = 1 + inner + halves - 1
+    kvw = keys.shape[1]
+    pages = owner.shape[1]
+    across = max(inner - 1, 1)
+    lines = outer if inner > 1 else 1
+    dma = pltpu.SemaphoreType.DMA
+    vmem = pl.BlockSpec(memory_space=pltpu.VMEM)
+    hbm = pl.BlockSpec(memory_space=pl.ANY)
+    return pl.pallas_call(
+        functools.partial(layer_kernel, outer, inner, halves, chunks),
+        out_shape=(
+            jax.ShapeDtypeStruct((tok, cols), BF16),
+            jax.ShapeDtypeStruct((pages * PAGE, 2 * kvw), BF16),
+        ),
+        in_specs=[hbm] + [vmem] * 11 + [hbm] * 3,
+        out_specs=(vmem, vmem),
+        scratch_shapes=[
+            pltpu.VMEM((peers, halves, tok, cols), BF16),
+            pltpu.VMEM((peers, tok, cols), BF16),
+            pltpu.VMEM((across, lines, tok, cols), BF16),
+            pltpu.VMEM((outer + 1, tok, cols), BF16),
+            pltpu.VMEM((experts * slots, width), BF16),
+            pltpu.VMEM((experts, width, 2 * ff), BF16),
+            pltpu.VMEM((experts, ff, width), BF16),
+            pltpu.VMEM((outer, experts, slots, ff), BF16),
+            pltpu.VMEM((experts * slots, inner * tok), BF16),
+            pltpu.VMEM((inner * tok, experts * slots), BF16),
+            pltpu.VMEM((inner * tok, 128), F32),
+            pltpu.VMEM((peers, meta_rows, tok), F32),
+            pltpu.VMEM((peers, meta_rows, tok), F32),
+            pltpu.VMEM((peers, PER_OWNER * PAGE, 2 * kvw), BF16),
+            pltpu.VMEM((peers, PER_OWNER * PAGE, 2 * kvw), BF16),
+            dma((kinds, peers)),
+            dma((peers, halves, chunks)),
+            dma((peers,)),
+            dma((peers,)),
+            dma((peers,)),
+            dma((peers,)),
+            dma((halves,)),
+            dma((2, experts)),
+            dma((experts,)),
+            dma((peers,)),
+            dma((peers,)),
+            dma((across, outer, chunks)),
+            dma((across, outer, chunks)),
+            dma((outer, chunks)),
+            dma((outer + 1, chunks)),
+        ],
+        compiler_params=pltpu.CompilerParams(
+            collective_id=0, has_side_effects=True, vmem_limit_bytes=LIMIT
+        ),
+        name="run_layer",
+    )(resid, gain, routes, gates, length, keys, values, kgain, cosine, sine, owner, page_slot, wg, wu, wd)
+
+
+def fits(outer, inner, halves, tok, width, experts, ff):
+    peers = outer * inner
+    block = tok * width // halves * 2
+    rows = (halves * peers + peers + outer * (inner - 1) + outer + 1) * block
+    return rows + 6 * experts * ff * width + 4 * experts * inner * CAP * width < LIMIT
+
+
 def inner_size(mesh):
     try:
         line = mesh.devices[0, :, 0]
@@ -763,6 +1299,15 @@
     halves = lax.axis_size("section")
     outer = lax.axis_size("ep") // inner
     cosine, sine = turns(resid.shape[0], k_gain.shape[0])
+    tok, width = resid.shape
+    if fits(outer, inner, halves, tok, width, w_gate.shape[0], w_gate.shape[2]):
+        moe_out, kv = run_layer(
+            outer, inner, halves,
+            resid, norm_gain[None, :], routes.T, gate_logits.T, lengths[None, :],
+            keys_raw, values_raw, k_gain[None, :], jnp.asarray(cosine), jnp.asarray(sine),
+            page_owner, page_slot, w_gate, w_up, w_down,
+        )
+        return (moe_out, kv.reshape(page_owner.shape[1], PAGE, 2, keys_raw.shape[1]))
     act, metas, kv = run_experts(
         outer, inner, halves,
         resid, norm_gain[None, :], routes, gate_logits, lengths[None, :],

time: 166 us -> 125 us (0.75)
  Pallas kernels: 156 us -> 118 us
  local copies, waits for them, and re-layouts: 7.63 us -> 4.79 us
    pallas_call x2 -> x1, Pallas kernels: 156 us -> 118 us  [run_layer(): pl.pallas_call(functools.partial(layer_kernel, outer, inner, halves, chun...]
    unnamed x3 -> x1, local copies, waits for them, and re-layouts: 4.71 us -> 1.88 us
where the time goes in v2:
time: 125 us; the launch traced here: 124 us
  Pallas kernels  118 us (94%)
  local copies, waits for them, and re-layouts  4.79 us (4%)
  between operations  1.29 us (1%)
    pallas_call x1, Pallas kernels, run_layer(): pl.pallas_call(functools.partial(layer_kernel, outer, inner, halves, chun...  118 us

profile of v2, /device:TPU:9, one launch (start us, length us, event | category | flops | bytes accessed | tf_op | source)
XLA Modules:
  0.0 124.5 jit_solution(17670306351350742767)
XLA Ops:
  1.3 1.3 %broadcast_in_dim.9.gain = bf16[1,4096]{1,0:T(2,128)(2,1)} reshape(bf16[4096]{0:T(1024)(128)(2,1)} %param.16) | data formatting | bytes 16384 | tf_op jit(solution)/shard_map/broadcast_in_dim | solution.py:1306
  2.6 118.4 %run_layer.1 = (bf16[128,2048]{1,0:T(8,128)(2,1)}, bf16[128,512]{1,0:T(8,128)(2,1)}) custom-call(bf16[128,4096]{1,0:T(8,128)(2,1)} %resid.1, bf16[1,4096]{1,0:T(2,128)(2,1)} %broadcast_in_dim.9.gain, s32[8,128]{1,0:T(8,128)} %bitcast.5, f32[8,128]{1,0:T(8,128)} %bitcast.6, s32[1,1]{1,0:T(1,128)} %bitcast.4.length, bf16[128,256]{1,0:T(8,128)(2,1)} %keys.1, ...), custom_call_target="tpu_custom_call" | custom-call | tf_op jit(solution)/shard_map/run_layer/pallas_call | solution.py:1203
  121.0 1.6 %reshape.7 = bf16[8,16,2,256]{3,2,1,0:T(2,128)(2,1)} reshape(bf16[128,512]{1,0:T(8,128)(2,1)} %get-tuple-element.5) | data formatting | bytes 262144 | tf_op jit(solution)/shard_map/reshape | solution.py:1310
  122.6 1.9 %copy.19 = bf16[128,2048]{1,0:T(8,128)(2,1)} copy(bf16[128,2048]{1,0:T(8,128)(2,1)} %get-tuple-element.8) | data formatting | bytes 1048576

commit v3 on v2

--- a/solution.py
+++ b/solution.py
@@ -725,8 +725,8 @@
     outer, inner, halves, chunks,
     resid, gain, routes, gates, length, keys, values, kgain, cosine, sine, owner, page_slot, wg, wu, wd,
     out, kv,
-    rows, sib, yb, zb, arrived, wbuf, dbuf, act, pick, comb, scale, metas, msend_buf, kvsend, kvrecv,
-    send, recv, msend, mrecv, ksend, krecv, local, wsem, dsem, ssend, srecv, ysend, yrecv, zsend, zrecv,
+    rows, sib, yb, zb, xb, arrived, wbuf, dbuf, act, pick, comb, scale, metas, msend_buf, kvsend, kvrecv,
+    send, recv, msend, mrecv, ksend, krecv, local, wsem, dsem, ssend, srecv, ysend, yrecv, zsend, zrecv, xsend, xrecv,
 ):
     ep, core, z, y = place(outer, inner)
     other = halves - 1 - core
@@ -741,6 +741,16 @@
     pages = owner.shape[1]
     kvw = keys.shape[1]
     tile = 512 if cols % 512 == 0 else 128
+    even = balanced(outer, inner)
+    low = chunks // 2
+    if even:
+        mate = z + 1 - 2 * lax.rem(z, 2)
+        skip = jnp.where(lax.rem(z, 2) == 0, outer - 1, 0)
+        mate_skip = outer - 1 - skip
+        is_end = (z == 0) | (z == outer - 1)
+        columns = [z, mate, lax.rem(z + 2, outer), outer - 1 - z]
+    else:
+        columns = [near_column(outer, z, i) for i in range(outer)]
 
     def remote(src, dst, send_sem, recv_sem, to_ep, to_core):
         return pltpu.make_async_remote_copy(
@@ -783,13 +793,13 @@
     pl.semaphore_wait(barrier, peers - 1 + 1)
 
     def chunk_copy(block, half, k, kind, to_ep, to_core):
-        at = (block, half, pl.ds(k * piece, piece), slice(None))
+        at = (block, half, pl.ds(pl.multiple_of(k * piece, piece), piece), slice(None))
         return remote(
             rows.at[at], rows.at[at], send.at[kind, block], recv.at[block, half, k], to_ep, to_core
         )
 
-    def block_sent(block, kind):
-        whole = rows.at[block, core]
+    def block_sent(block, kind, amount=chunks):
+        whole = rows.at[block, core, pl.ds(0, amount * piece)]
         remote(whole, whole, send.at[kind, block], recv.at[block, core, 0], ep, other).wait_send()
 
     def landed(block, half, k):
@@ -915,7 +925,7 @@
             total = total + jnp.dot(where, kvrecv[source], preferred_element_type=F32)
         kv[...] = total.astype(BF16)
 
-    def step(d):
+    def step(d, first=0, last=chunks):
         def body(k, carry):
             def one(side, zz):
                 block = zz * inner + y
@@ -924,13 +934,25 @@
                     pl.when(z > 0)(lambda: to_down(block, k))
                 else:
                     pl.when(z < outer - 1)(lambda: to_up(block, k))
-                to_across(block, k)
+                if even:
+                    late = jnp.logical_not(is_end) & (zz == columns[3])
+                    pl.when(jnp.logical_not(late | ((zz == skip) & (k >= low))))(
+                        lambda: to_across(block, k)
+                    )
+                else:
+                    to_across(block, k)
                 to_sibling(block, k)
 
             sides(outer, z, d, one)
             return carry
 
-        lax.fori_loop(0, chunks, body, 0)
+        lax.fori_loop(first, last, body, 0)
+        if even and d == 2:
+
+            @pl.when(jnp.logical_not(is_end))
+            def _():
+                for k in range(chunks):
+                    to_across(columns[3] * inner + y, k)
 
     def across(zz):
         def body(k, carry):
@@ -938,6 +960,10 @@
                 block = zz * inner + lax.rem(y + n, inner)
                 landed(block, core, k)
                 to_sibling(block, k)
+                if even:
+                    around = (zz == mate_skip) & (k >= low)
+                    pl.when(around & (mate < z))(lambda: to_down(block, k))
+                    pl.when(around & (mate > z))(lambda: to_up(block, k))
             return carry
 
         lax.fori_loop(0, chunks, body, 0)
@@ -967,14 +993,43 @@
 
         lax.fori_loop(0, chunks, body, 0)
 
+    def matches(zz):
+        meta = [metas[zz * inner + p] for p in range(inner)]
+        return meta, slot_match(meta, 0, experts, slots, inner)
+
+    def choose(zz):
+        match = matches(zz)[1]
+        for j in range(experts):
+            for p in range(inner):
+                pick[j * slots : (j + 1) * slots, p * tok : (p + 1) * tok] = jnp.where(
+                    match[j][p], 1.0, 0.0
+                ).astype(BF16)
+
+    def weigh(zz):
+        meta, match = matches(zz)
+        for p in range(inner):
+            weights = [
+                jnp.where(match[j][p], meta[p][experts + j : experts + j + 1, :], 0.0)
+                for j in range(experts)
+            ]
+            comb[p * tok : (p + 1) * tok, :] = jnp.concatenate(weights, axis=0).T.astype(BF16)
+
+    def prepare(i):
+        for p in range(inner):
+            block = columns[i] * inner + p
+            if i == 0:
+                pl.when(block != ep)(functools.partial(meta_landed, block))
+            else:
+                meta_landed(block)
+        choose(columns[i])
+        if even and i > 0:
+            weigh(columns[i])
+
     def hidden_layer(zz, own):
         for n in range(inner):
             p = lax.rem(y + n, inner)
             block = zz * inner + p
             other_half(block, p, own and n == 0)
-            if own and n == 0:
-                continue
-            meta_landed(block)
         meta = [metas[zz * inner + p] for p in range(inner)]
         match = slot_match(meta, 0, experts, slots, inner)
         factors = []
@@ -984,9 +1039,6 @@
         for j in range(experts):
             factor = jnp.zeros((slots, 1), F32)
             for p in range(inner):
-                pick[j * slots : (j + 1) * slots, p * tok : (p + 1) * tok] = jnp.where(
-                    match[j][p], 1.0, 0.0
-                ).astype(BF16)
                 factor = factor + jnp.sum(
                     jnp.where(match[j][p], lanes[p], 0.0), axis=-1, keepdims=True
                 )
@@ -999,7 +1051,7 @@
                 to = pl.ds(pl.multiple_of(h * cols + i * span, span), span)
                 source = rows[pl.ds(zz * inner, inner), h, :, at].reshape(inner * tok, span)
                 found = jnp.dot(pick[...], source, preferred_element_type=F32)
-                arrived[:, to] = (found * factor * gain[:, to].astype(F32)).astype(BF16)
+                arrived[:, to] = (found * factor * gain[to].astype(F32)[None, :]).astype(BF16)
                 return carry
 
             lax.fori_loop(0, cols // span, select, 0)
@@ -1018,14 +1070,21 @@
 
     def y_copy(zz, n, k):
         to_y = lax.rem(y + n, inner)
-        at = pl.ds(k * piece, piece)
+        at = pl.ds(pl.multiple_of(k * piece, piece), piece)
         return remote(
             rows.at[zz * inner + to_y, core, at], yb.at[n - 1, zz, at],
             ysend.at[n - 1, zz, k], yrecv.at[n - 1, zz, k], z * inner + to_y, core,
         )
 
+    def x_copy(k):
+        at = pl.ds(pl.multiple_of(k * piece, piece), piece)
+        return remote(
+            rows.at[mate * inner + lax.rem(y + 1, inner), core, at], xb.at[at],
+            xsend.at[k], xrecv.at[k], mate * inner + y, core,
+        )
+
     def z_copy(zz, slot, to_ep, k):
-        at = pl.ds(k * piece, piece)
+        at = pl.ds(pl.multiple_of(k * piece, piece), piece)
         return remote(
             rows.at[zz * inner + y, core, at], zb.at[slot, at],
             zsend.at[zz, k], zrecv.at[slot, k], to_ep, core,
@@ -1051,17 +1110,17 @@
             pl.when(same & (z > 0) & (zz >= z))(functools.partial(block_sent, block, 0))
             pl.when(same & (z < outer - 1) & (zz <= z))(functools.partial(block_sent, block, 1))
             for n in range(1, inner):
-                pl.when(same)(functools.partial(block_sent, block, 1 + n))
+                if even:
+                    pl.when(same & (zz != skip))(functools.partial(block_sent, block, 1 + n))
+                    pl.when(same & (zz == skip))(functools.partial(block_sent, block, 1 + n, low))
+                else:
+                    pl.when(same)(functools.partial(block_sent, block, 1 + n))
+            if even:
+                around = (y != p) & (zz == mate_skip)
+                rest = chunks - low
+                pl.when(around & (mate < z))(functools.partial(block_sent, block, 0, rest))
+                pl.when(around & (mate > z))(functools.partial(block_sent, block, 1, rest))
             pl.when(block != ep)(functools.partial(block_sent, block, sib_kind))
-        meta = [metas[zz * inner + p] for p in range(inner)]
-        match = slot_match(meta, 0, experts, slots, inner)
-        for p in range(inner):
-            weights = [
-                jnp.where(match[j][p], meta[p][experts + j : experts + j + 1, :], 0.0)
-                for j in range(experts)
-            ]
-            comb[p * tok : (p + 1) * tok, :] = jnp.concatenate(weights, axis=0).T.astype(BF16)
-
         def half_of(half, to_sib):
             at = pl.ds(pl.multiple_of(half * cols, cols), cols)
 
@@ -1072,7 +1131,7 @@
                 ).astype(BF16)
                 return carry
 
-            lax.fori_loop(0, experts, expert, 0)
+            lax.fori_loop(0, experts, expert, 0, unroll=True)
             span = min(cols, MIX)
 
             def body(i, carry):
@@ -1091,35 +1150,60 @@
         half_of(other, True)
         half_of(core, False)
 
-    def hand_across(zz):
+    def hand_across(zz, how="y"):
         for n in range(1, inner):
             block = zz * inner + lax.rem(y + n, inner)
+            mine = rows.at[block, core]
             sib_copy(block).wait_recv()
-            for k in range(chunks):
-                add(rows.at[block, core], k, rows.at[block, core], sib.at[block])
-                y_copy(zz, n, k).start()
-
-    def z_step(d, side, zz):
-        block = zz * inner + y
-        mine = rows.at[block, core]
-        sib_copy(block).wait_recv()
-        for k in range(chunks):
-            for n in range(1, inner):
-                y_copy(zz, n, k).wait_recv()
-            parts = [mine, sib.at[block]] + [yb.at[n, zz] for n in range(inner - 1)]
-            feeds = (z - side >= 0) & (z - side < outer)
-            slot = outer if (d == 1 and side == -1) else zz
-
-            @pl.when(feeds)
+
+            def body(k, carry):
+                if how == "merge":
+                    x_copy(k).wait_recv()
+                    add(mine, k, mine, sib.at[block], xb)
+                else:
+                    add(mine, k, mine, sib.at[block])
+                if how == "x":
+                    x_copy(k).start()
+                else:
+                    y_copy(zz, n, k).start()
+                return carry
+
+            lax.fori_loop(0, chunks, body, 0)
+
+    def z_step(*targets):
+        for zz in targets:
+            sib_copy(zz * inner + y).wait_recv()
+
+        def one(zz, k):
+            block = zz * inner + y
+            mine = rows.at[block, core]
+            up = zz > z
+            feeds = jnp.where(up, z > 0, z < outer - 1)
+            ends = jnp.logical_not(feeds)
+            ahead = jnp.where(up, z + 1, z - 1)
+            slot = jnp.where((ahead == zz) & (zz < z), outer, zz)
+            with_y = zz != mate if even else zz != z
+            without = jnp.logical_not(with_y)
+            others = [yb.at[n, zz] for n in range(inner - 1)]
+
+            @pl.when(with_y)
             def _():
-                z_copy(zz, zz, ep, k).wait_recv()
-                add(mine, k, *parts, zb.at[zz])
-
-            @pl.when(jnp.logical_not(feeds))
-            def _():
-                add(mine, k, *parts)
-
-            z_copy(zz, slot, ep + side * inner, k).start()
+                for n in range(1, inner):
+                    y_copy(zz, n, k).wait_recv()
+
+            pl.when(feeds)(lambda: z_copy(zz, zz, ep, k).wait_recv())
+            pl.when(feeds & with_y)(lambda: add(mine, k, mine, sib.at[block], *others, zb.at[zz]))
+            pl.when(ends & with_y)(lambda: add(mine, k, mine, sib.at[block], *others))
+            pl.when(feeds & without)(lambda: add(mine, k, mine, sib.at[block], zb.at[zz]))
+            pl.when(ends & without)(lambda: add(mine, k, mine, sib.at[block]))
+            z_copy(zz, slot, ahead * inner + y, k).start()
+
+        def body(k, carry):
+            for zz in targets:
+                one(zz, k)
+            return carry
+
+        lax.fori_loop(0, chunks, body, 0)
 
     def last_step():
         sib_copy(ep).wait_recv()
@@ -1135,37 +1219,81 @@
             pl.when((z == 0) & (z < outer - 1))(lambda: add(out, k, *parts, zb.at[outer]))
             pl.when((z > 0) & (z == outer - 1))(lambda: add(out, k, *parts, zb.at[z]))
 
-    columns = [near_column(outer, z, i) for i in range(outer)]
     prepare_pages()
-    for i in range(outer):
-        if i + 1 < outer:
-            step(i + 1)
-        if i == max(outer - 2, 0):
-            for n in range(1, peers):
-                kv_copy(n).start()
-        across(columns[i])
+    def send_pages():
+        for n in range(1, peers):
+            kv_copy(n).start()
+
+    def wait_weights(i):
         if i == 0:
             for j in range(experts):
                 for which in range(2):
                     w_copy(j, which).wait()
+
+    middle = jnp.logical_not(is_end) if even else None
+    for i in range(outer):
+        if i + 1 < outer and not (even and i == 2):
+            step(i + 1)
+        if even and i == 2:
+
+            @pl.when(is_end)
+            def _():
+                step(3, low)
+                across(columns[2])
+
+        prepare(i)
+        if not (even and i == 2):
+            across(columns[i])
+        if i == outer - 1:
+            send_pages()
+        wait_weights(i)
         hidden_layer(columns[i], i == 0)
         if i == 0:
             for j in range(experts):
                 d_copy(j).wait()
-        if i == 1 and outer > 2:
-            output_layer(columns[0])
-        if i >= outer - 2:
+        if even and i == 1:
+            pl.when(is_end)(lambda: step(3, 0, low))
+            pl.when(middle)(lambda: across(columns[2]))
+            output_layer(mate)
+
+            @pl.when(is_end)
+            def _():
+                hand_across(mate, "x")
+                z_step(mate)
+        elif even and i > 1:
             output_layer(columns[i])
             hand_across(columns[i])
-    for i in range(outer - 3, -1, -1):
-        if i > 0 or outer <= 2:
+            if i == 2:
+                pl.when(middle)(lambda: hand_across(mate, "x"))
+        elif not even and i >= outer - 2:
+            weigh(columns[i])
             output_layer(columns[i])
-        hand_across(columns[i])
-    for d in range(outer - 1, 0, -1):
-        sides(outer, z, d, functools.partial(z_step, d))
-        if d == outer - 1:
-            place_pages()
+            hand_across(columns[i])
+    if even:
+        weigh(columns[0])
+        pl.when(is_end)(lambda: z_step(columns[2]))
+        output_layer(columns[0])
+        hand_across(columns[0], "merge")
+        pl.when(is_end)(lambda: z_step(columns[3]))
+
+        @pl.when(middle)
+        def _():
+            z_step(columns[2])
+            z_step(mate, columns[3])
+
+        place_pages()
+    else:
+        for i in range(outer - 3, -1, -1):
+            weigh(columns[i])
+            output_layer(columns[i])
+            hand_across(columns[i])
+        for d in range(outer - 1, 0, -1):
+            sides(outer, z, d, lambda side, zz: z_step(zz))
+        place_pages()
     last_step()
+
+    def y_sent(zz, n, k):
+        y_copy(zz, n, k).wait_send()
 
     for d in range(outer - 1, 0, -1):
         def sent(side, zz):
@@ -1176,12 +1304,22 @@
     for zz in range(outer):
         for n in range(1, inner):
             for k in range(chunks):
-                y_copy(zz, n, k).wait_send()
+                if even:
+                    pl.when(mate != zz)(functools.partial(y_sent, zz, n, k))
+                else:
+                    y_sent(zz, n, k)
+    if even:
+        for k in range(chunks):
+            x_copy(k).wait_send()
     for block in range(peers):
         sib_copy(block).wait_send()
     for n in range(1, peers):
         meta_copy(n).wait_send()
         kv_copy(n).wait_send()
+
+
+def balanced(outer, inner):
+    return outer == 4 and inner == 2
 
 
 def run_layer(outer, inner, halves, resid, gain, routes, gates, length, keys, values, kgain, cosine, sine, owner, page_slot, wg, wu, wd):
@@ -1213,6 +1351,7 @@
             pltpu.VMEM((peers, tok, cols), BF16),
             pltpu.VMEM((across, lines, tok, cols), BF16),
             pltpu.VMEM((outer + 1, tok, cols), BF16),
+            pltpu.VMEM((tok, cols) if balanced(outer, inner) else (16, 128), BF16),
             pltpu.VMEM((experts * slots, width), BF16),
             pltpu.VMEM((experts, width, 2 * ff), BF16),
             pltpu.VMEM((experts, ff, width), BF16),
@@ -1239,6 +1378,8 @@
             dma((across, outer, chunks)),
             dma((outer, chunks)),
             dma((outer + 1, chunks)),
+            dma((chunks,)),
+            dma((chunks,)),
         ],
         compiler_params=pltpu.CompilerParams(
             collective_id=0, has_side_effects=True, vmem_limit_bytes=LIMIT
@@ -1303,7 +1444,7 @@
     if fits(outer, inner, halves, tok, width, w_gate.shape[0], w_gate.shape[2]):
         moe_out, kv = run_layer(
             outer, inner, halves,
-            resid, norm_gain[None, :], routes.T, gate_logits.T, lengths[None, :],
+            resid, norm_gain, routes.T, gate_logits.T, lengths[None, :],
             keys_raw, values_raw, k_gain[None, :], jnp.asarray(cosine), jnp.asarray(sine),
             page_owner, page_slot, w_gate, w_up, w_down,
         )

time: 125 us -> 117 us (0.936)
  Pallas kernels: 118 us -> 111 us
  local copies, waits for them, and re-layouts: 4.79 us -> 3.47 us
    pallas_call x1, Pallas kernels: 118 us -> 111 us  [run_layer(): pl.pallas_call(functools.partial(layer_kernel, outer, inner, halves, chun...]
    broadcast_in_dim x1 -> x0, local copies, waits for them, and re-layouts: 1.31 us -> none  [shards(): norm_gain[None, :]]
where the time goes in v3:
time: 117 us; the launch traced here: 116 us
  Pallas kernels  111 us (95%)
  local copies, waits for them, and re-layouts  3.47 us (3%)
  between operations  1.29 us (1%)
    pallas_call x1, Pallas kernels, run_layer(): pl.pallas_call(functools.partial(layer_kernel, outer, inner, halves, chun...  111 us

profile of v3, /device:TPU:9, one launch (start us, length us, event | category | flops | bytes accessed | tf_op | source)
XLA Modules:
  0.0 115.7 jit_solution(17030333495444918964)
XLA Ops:
  1.3 110.9 %run_layer.1 = (bf16[128,2048]{1,0:T(8,128)(2,1)}, bf16[128,512]{1,0:T(8,128)(2,1)}) custom-call(bf16[128,4096]{1,0:T(8,128)(2,1)} %resid.1, bf16[4096]{0:T(1024)(128)(2,1)} %gain.1, s32[8,128]{1,0:T(8,128)} %bitcast.5, f32[8,128]{1,0:T(8,128)} %bitcast.6, s32[1,1]{1,0:T(1,128)} %bitcast.4.length, bf16[128,256]{1,0:T(8,128)(2,1)} %keys.1, ...), custom_call_target="tpu_custom_call" | custom-call | tf_op jit(solution)/shard_map/run_layer/pallas_call | solution.py:1341
  112.2 1.6 %reshape.7 = bf16[8,16,2,256]{3,2,1,0:T(2,128)(2,1)} reshape(bf16[128,512]{1,0:T(8,128)(2,1)} %get-tuple-element.5) | data formatting | bytes 262144 | tf_op jit(solution)/shard_map/reshape | solution.py:1451
  113.8 1.9 %copy.19 = bf16[128,2048]{1,0:T(8,128)(2,1)} copy(bf16[128,2048]{1,0:T(8,128)(2,1)} %get-tuple-element.8) | data formatting | bytes 1048576
